TPU v7x, 32 devices: a whole 2x2x4 slice. The times are simulated.
32 devices in a mesh: ez: 4 (over z), ey: 2 (over y), ex: 4 (over x, core).
Axes of the slice: x: 2, y: 2, z: 4, core: 2. Of those that a mesh axis runs over, the one named last changes fastest.
Arguments:
- tokens: bfloat16 [8192, 2048], P(('ez', 'ey', 'ex'))
- expert_ids: int32 [8192, 8], P(('ez', 'ey', 'ex'))
- gate_weights: float32 [8192, 8], P(('ez', 'ey', 'ex'))
- w_gate: bfloat16 [128, 2048, 768], P(('ez', 'ey', 'ex'))
- w_up: bfloat16 [128, 2048, 768], P(('ez', 'ey', 'ex'))
- w_down: bfloat16 [128, 768, 2048], P(('ez', 'ey', 'ex'))
Outputs:
- output: bfloat16 [8192, 2048], P(('ez', 'ey', 'ex'))
All inputs are finite; a program needn't handle non-finite values.
Results may differ from a plain program's by a relative error of at most 0.00586641.
Values are sent between devices in bfloat16 or wider.
A program may use at most 1 GiB of HBM per device.

v0:
```python
import math
import jax
import jax.numpy as jnp
from jax import lax
from jax.sharding import PartitionSpec as P


def pack_rows(chosen, gate_vals, per_expert):
    row_rank = jnp.cumsum(chosen.astype(jnp.int32), axis=0) - 1
    slot_idx = jnp.where(chosen, row_rank, per_expert)
    row_idx = jnp.broadcast_to(jnp.arange(chosen.shape[0])[:, None], chosen.shape)
    exp_idx = jnp.broadcast_to(jnp.arange(chosen.shape[1])[None, :], chosen.shape)
    pick_rows = jnp.zeros((chosen.shape[1], per_expert), jnp.int32).at[exp_idx, slot_idx].set(row_idx, mode="drop")
    pick_gates = jnp.zeros((chosen.shape[1], per_expert), jnp.float32).at[exp_idx, slot_idx].set(gate_vals, mode="drop")
    return pick_rows, pick_gates


def expert_ffn(x_pack, w_gate, w_up, w_down, pick_gates):
    gate_act = jnp.einsum("lch,lhf->lcf", x_pack, w_gate, preferred_element_type=jnp.float32)
    up_act = jnp.einsum("lch,lhf->lcf", x_pack, w_up, preferred_element_type=jnp.float32)
    hidden_act = (jax.nn.silu(gate_act) * up_act).astype(jnp.bfloat16)
    expert_out = jnp.einsum("lcf,lfh->lch", hidden_act, w_down, preferred_element_type=jnp.float32)
    return expert_out * pick_gates[:, :, None]


def solution(mesh):
    ep_axes = tuple(mesh.axis_names)
    num_devices = math.prod(mesh.shape[axis_name] for axis_name in ep_axes)
    row_spec = P(ep_axes, None)
    w_spec = P(ep_axes, None, None)

    def local_layer(tokens, expert_ids, gate_weights, w_gate, w_up, w_down):
        tok_dev, hidden = tokens.shape
        top_k = expert_ids.shape[1]
        local_experts = w_gate.shape[0]
        capacity = tok_dev * top_k // num_devices
        rows_recv = num_devices * capacity
        per_expert = rows_recv // local_experts
        dest_dev = expert_ids // local_experts
        dev_hit = jnp.any(dest_dev[:, :, None] == jnp.arange(num_devices)[None, None, :], axis=1)
        all_experts = jnp.arange(num_devices * local_experts)
        gate_dense = jnp.sum(jnp.where(expert_ids[:, :, None] == all_experts[None, None, :], gate_weights[:, :, None], 0.0), axis=1)
        gate_dense = gate_dense.reshape(tok_dev, num_devices, local_experts)
        slot_pos = jnp.cumsum(dev_hit.astype(jnp.int32), axis=0) - 1
        place_mask = dev_hit[:, :, None] & (slot_pos[:, :, None] == jnp.arange(capacity)[None, None, :])
        place_bf = place_mask.astype(jnp.bfloat16)
        send_rows = jnp.einsum("tdc,th->dch", place_bf, tokens, preferred_element_type=jnp.float32).astype(jnp.bfloat16)
        send_gates = jnp.sum(jnp.where(place_mask[:, :, :, None], gate_dense[:, :, None, :], 0.0), axis=0)
        recv_rows = lax.all_to_all(send_rows, ep_axes, 0, 0, tiled=True)
        recv_gates = lax.all_to_all(send_gates, ep_axes, 0, 0, tiled=True)
        flat_rows = recv_rows.reshape(rows_recv, hidden)
        flat_gates = recv_gates.reshape(rows_recv, local_experts)
        pick_rows, pick_gates = pack_rows(flat_gates > 0.0, flat_gates, per_expert)
        weighted = expert_ffn(flat_rows[pick_rows], w_gate, w_up, w_down, pick_gates)
        part_sum = jax.ops.segment_sum(weighted.reshape(-1, hidden), pick_rows.reshape(-1), num_segments=rows_recv)
        back_rows = part_sum.astype(jnp.bfloat16).reshape(num_devices, capacity, hidden)
        returned = lax.all_to_all(back_rows, ep_axes, 0, 0, tiled=True)
        moe_sum = jnp.einsum("tdc,dch->th", place_bf, returned, preferred_element_type=jnp.float32)
        return (tokens.astype(jnp.float32) + moe_sum).astype(jnp.bfloat16)

    return jax.shard_map(local_layer, mesh=mesh, in_specs=(row_spec, row_spec, row_spec, w_spec, w_spec, w_spec), out_specs=row_spec, check_vma=False)
```

profile of v0, /device:TPU:0, one launch (start us, length us, event | category | flops | bytes accessed | tf_op | source)
XLA Modules:
  0.0 504.8 jit_solution(10610896463060978711)
XLA Ops:
  0.0 0.7 add_select_fusion
  0.7 0.8 copy.49
  1.6 0.6 reduce-window.14
  2.2 0.2 slice_reduce_fusion.1
  2.4 0.1 bitcast_bitcast_fusion.1
  2.5 0.8 copy.50
  3.3 1.3 select_reduce_fusion.1
  4.6 0.1 copy.51
  4.7 0.5 fusion.7
  5.2 1.2 select_reduce_fusion
  6.4 0.7 reshape.122
  7.1 7.4 %all-to-all-start = ((f32[32,1,256]{2,1,0:T(1,128)}), f32[32,1,256]{2,1,0:T(1,128)S(1)}, u32[]{:S(2)}, u32[]{:S(2)}) async-start(f32[32,1,256]{2,1,0:T(1,128)} %reshape.122), calls=%async_computation | async-start | bytes 65536 | tf_op jit(solution)/shard_map/all_to_all | solution.py:50
  14.5 6.8 %convolution_convert_fusion = bf16[32,64,2048]{2,1,0:T(8,128)(2,1)} fusion(bf16[256,2048]{1,0:T(8,128)(2,1)} %param.6, s32[256,32]{0,1:T(8,128)S(1)} %bitcast_bitcast_fusion.1, pred[256,32]{0,1:T(8,128)(4,1)S(1)} %fusion.9), kind=kOutput, calls=%fused_computation.9 | convolution fusion | flops 2152726528 | bytes 9478144 | tf_op jit(solution)/shard_map/tdc,th->dch/dot_general | solution.py:47
  21.3 0.0 copy-start.2
  21.3 0.0 copy-start.1
  21.3 0.3 all-to-all-done
  21.6 5.7 %all-to-all-start.1 = ((bf16[32,64,2048]{2,1,0:T(8,128)(2,1)}), bf16[32,64,2048]{2,1,0:T(8,128)(2,1)}, u32[]{:S(2)}, u32[]{:S(2)}) async-start(bf16[32,64,2048]{2,1,0:T(8,128)(2,1)} %convolution_convert_fusion), calls=%async_computation.1 | async-start | bytes 16777216 | tf_op jit(solution)/shard_map/all_to_all | solution.py:49
  27.3 0.1 broadcast_in_dim.85
  27.3 0.6 reshape.96
  28.0 0.5 broadcast.122
  28.5 0.7 reduce.10
  29.2 0.1 reshape.123
  29.3 0.4 copy.54
  29.7 0.1 reshape.111
  29.9 1.2 reduce-window.16
  31.0 0.2 slice_reduce_fusion
  31.2 0.2 reduce-window.19
  31.4 0.7 reshape.102
  32.1 0.1 add_bitcast_fusion
  32.2 0.0 copy-done.2
  32.2 0.1 multiply_reduce_fusion
  32.3 0.0 copy-done.1
  32.3 0.1 and_reduce_fusion
  32.5 0.4 copy.53
  32.8 0.6 reshape.94
  33.5 30.4 %scatter_custom_fusion.2 = f32[2048]{0:T(1024)S(1)} fusion(s32[8192]{0:T(1024)S(1)} %reshape.94, f32[8192]{0:T(1024)S(1)} %reshape.102, f32[]{:T(128)} %constant.41.clone.1), kind=kCustom, calls=%fused_computation.50 | custom fusion | bytes 8196
  63.9 30.6 %scatter_custom_fusion.1 = s32[2048]{0:T(1024)S(1)} fusion(s32[8192]{0:T(1024)S(1)} %reshape.94, s32[8192]{0:T(1024)S(1)} %reshape.96, s32[]{:T(128)} %constant.20.clone.1), kind=kCustom, calls=%fused_computation.52 | custom fusion | bytes 8196 | tf_op jit(solution)/shard_map/broadcast_in_dim;reshape | solution.py:55
  94.6 108.8 %all-to-all-done.1 = bf16[32,64,2048]{2,1,0:T(8,128)(2,1)} async-done(((bf16[32,64,2048]{2,1,0:T(8,128)(2,1)}), bf16[32,64,2048]{2,1,0:T(8,128)(2,1)}, u32[]{:S(2)}, u32[]{:S(2)}) %all-to-all-start.1) | async-done | bytes 8388640 | tf_op jit(solution)/shard_map/all_to_all | solution.py:49
  203.4 20.8 %gather_fusion = bf16[2048,2048]{1,0:T(8,128)(2,1)} fusion(bf16[2048,2048]{1,0:T(8,128)(2,1)} %bitcast.6, s32[2048]{0:T(1024)S(1)} %broadcast_clamp_fusion), kind=kCustom, calls=%fused_computation | custom fusion | bytes 16785408 | tf_op jit(solution)/shard_map/gather | solution.py:54
  224.2 14.4 %fusion.22 = f32[4,512,768]{2,1,0:T(8,128)} fusion(bf16[4,512,2048]{2,1,0:T(8,128)(2,1)} %bitcast.67, bf16[4,2048,768]{2,1,0:T(8,128)(2,1)} %param.9), kind=kOutput, calls=%fused_computation.55 | convolution fusion | flops 6442450944 | bytes 27262976 | tf_op jit(solution)/shard_map/lch,lhf->lcf/dot_general | solution.py:19
  238.6 24.3 %broadcast_multiply_fusion = f32[4,512,2048]{2,1,0:T(8,128)} fusion(f32[4,512]{1,0:T(4,128)S(1)} %reshape.74, bf16[4,768,2048]{2,1,0:T(8,128)(2,1)} %param.11, f32[4,512,768]{2,1,0:T(8,128)} %fusion.22, bf16[4,512,2048]{2,1,0:T(8,128)(2,1)} %bitcast.68, bf16[4,2048,768]{2,1,0:T(8,128)(2,1)} %param.10), kind=kOutput, calls=%fused_computation.4 | convolution fusion | flops 12898533376 | bytes 56631296 | tf_op jit(solution)/shard_map/lcf,lfh->lch/dot_general | solution.py:22
  262.9 34.1 %scatter_custom_fusion = f32[2048,2048]{1,0:T(8,128)} fusion(s32[2048]{0:T(1024)S(1)} %scatter_custom_fusion.1, f32[2048,2048]{1,0:T(8,128)} %bitcast.75, f32[]{:T(128)} %constant.41.clone.1), kind=kCustom, calls=%fused_computation.6 | custom fusion | flops 4194304 | bytes 16777728 | tf_op jit(solution)/shard_map/scatter-add | solution.py:55
  297.0 6.5 %convert_element_type.26 = bf16[2048,2048]{1,0:T(8,128)(2,1)S(1)} convert(f32[2048,2048]{1,0:T(8,128)} %scatter_custom_fusion) | non-fusion elementwise | flops 4194304 | bytes 25165824 | tf_op jit(solution)/shard_map/convert_element_type | solution.py:56
  303.5 0.0 copy-start
  303.5 197.9 %all_to_all.15 = bf16[32,64,2048]{2,1,0:T(8,128)(2,1)S(1)} all-to-all(bf16[32,64,2048]{2,1,0:T(8,128)(2,1)S(1)} %bitcast.66), channel_id=1, replica_groups=mesh['ez'=4,'ey'=2,'ex'=4] {'ez','ey','ex'}, dimensions={0} | all-to-all | bytes 16777216 | tf_op jit(solution)/shard_map/all_to_all | solution.py:57
  501.4 0.0 copy-done
  501.4 3.4 fusion.6
  (16 shorter events, 0.2 us)
Async XLA Ops:
  7.1 14.5 %all-to-all-start = ((f32[32,1,256]{2,1,0:T(1,128)}), f32[32,1,256]{2,1,0:T(1,128)S(1)}, u32[]{:S(2)}, u32[]{:S(2)}) async-start(f32[32,1,256]{2,1,0:T(1,128)} %reshape.122), calls=%async_computation | async-start | bytes 65536 | tf_op jit(solution)/shard_map/all_to_all | solution.py:50
  21.3 10.9 %copy-start.2 = (s32[2]{0:T(128)S(1)}, s32[2]{0:T(128)}, u32[]{:S(2)}) copy-start(s32[2]{0:T(128)} %constant.48) | copy-start | bytes 28
  21.3 11.0 %copy-start.1 = (s32[2]{0:T(128)S(1)}, s32[2]{0:T(128)}, u32[]{:S(2)}) copy-start(s32[2]{0:T(128)} %constant.51) | copy-start | bytes 28
  21.6 181.8 %all-to-all-start.1 = ((bf16[32,64,2048]{2,1,0:T(8,128)(2,1)}), bf16[32,64,2048]{2,1,0:T(8,128)(2,1)}, u32[]{:S(2)}, u32[]{:S(2)}) async-start(bf16[32,64,2048]{2,1,0:T(8,128)(2,1)} %convolution_convert_fusion), calls=%async_computation.1 | async-start | bytes 16777216 | tf_op jit(solution)/shard_map/all_to_all | solution.py:49
  303.5 197.9 %copy-start = (bf16[256,2048]{1,0:T(8,128)(2,1)S(1)}, bf16[256,2048]{1,0:T(8,128)(2,1)}, u32[]{:S(2)}) copy-start(bf16[256,2048]{1,0:T(8,128)(2,1)} %param.6) | copy-start | bytes 3145732
where the time goes:
time: 506 us; the launch traced here: 505 us
  blocking collectives  198 us (39%)
  waiting for transfers between devices  109 us (22%)
  local copies, waits for them, and re-layouts  88.3 us (17%)
  matrix products  48.8 us (10%)
  other arithmetic  47.4 us (9%)
  starting transfers between devices  13 us (3%)
    all_to_all x1, blocking collectives, local_layer(): returned = lax.all_to_all(back_rows, ep_axes, 0, 0, tiled=True)  198 us
    all_to_all x1, waiting for transfers between devices, local_layer(): recv_rows = lax.all_to_all(send_rows, ep_axes, 0, 0, tiled=True)  109 us
    scatter-add x1, other arithmetic, local_layer(): jax.ops.segment_sum(weighted.reshape(-1, hidden), pick_rows.reshape(-1),...  34.1 us
    unnamed x15, local copies, waits for them, and re-layouts  33.9 us
    another operation x1, local copies, waits for them, and re-layouts, local_layer(): jax.ops.segment_sum(weighted.reshape(-1, hidden), pick_rows.reshape(-1),...  30.6 us
    dot_general x1, matrix products, expert_ffn(): jnp.einsum('lcf,lfh->lch', hidden_act, w_down, preferred_element_type=jnp...  24.3 us
    gather x1, local copies, waits for them, and re-layouts, local_layer(): flat_rows[pick_rows]  20.8 us
    dot_general x1, matrix products, expert_ffn(): jnp.einsum('lch,lhf->lcf', x_pack, w_gate, preferred_element_type=jnp.flo...  14.4 us
  transfers between devices with their start and end apart: 2, of which 2 were waited for; matrix products, arithmetic and copies ran while one was open for 15% of the time, Pallas kernels for 0%

commit v1 on v0

v1 whole, which is shorter than its diff:
```python
import functools
import math

import jax
import jax.numpy as jnp
from jax import lax
from jax.experimental import pallas as pl
from jax.experimental.pallas import tpu as pltpu
from jax.sharding import PartitionSpec as P

MESH = pl.DeviceIdType.MESH
F32 = jnp.float32
BF16 = jnp.bfloat16


def routing_tables(expert_ids, gate_weights, num_devices, local_experts, capacity):
    tok_dev = expert_ids.shape[0]
    dev_hit = jnp.any((expert_ids // local_experts)[:, :, None] == jnp.arange(num_devices)[None, None, :], axis=1)
    slot_pos = jnp.where(dev_hit, jnp.cumsum(dev_hit.astype(jnp.int32), axis=0) - 1, -1)
    all_experts = jnp.arange(num_devices * local_experts)
    gate_dense = jnp.sum(jnp.where(expert_ids[:, :, None] == all_experts[None, None, :], gate_weights[:, :, None], 0.0), axis=1)
    gate_dense = gate_dense.reshape(tok_dev, num_devices, local_experts)
    place = slot_pos[:, :, None] == jnp.arange(capacity)[None, None, :]
    slot_gates = jnp.sum(jnp.where(place[:, :, None, :], gate_dense[:, :, :, None], 0.0), axis=0)
    return slot_pos.T, slot_gates


def moe_kernel(
    dims, x_ref, slot_ref, sgate_ref, w1_ref, w3_ref, w2_ref, out_ref,
    xall, smap, grecv, place, sbuf, drecv, rrecv, zret, acc, hbuf, gb, wb1, wb3, wb2,
    x_sem, w_sem, zs_send, zs_recv, sm_send, sm_recv, g_send, g_recv, d_send, d_recv, r_send, r_recv, zr_send, zr_recv,
):
    nz, ny, nx = dims
    nq = ny * nx
    ndev = nz * nq
    tok, hid = xall.shape[1:]
    cap = sbuf.shape[2]
    ff = wb1.shape[2]
    rows = nq * cap
    nt = 256
    ft = 256
    z = lax.axis_index("ez")
    q = lax.axis_index("ey") * nx + lax.axis_index("ex")
    me = z * nq + q

    def at(zz, qq):
        return (zz, lax.div(qq, nx), lax.rem(qq, nx))

    def rcopy(src, dst, ss, rs, dev):
        return pltpu.make_async_remote_copy(src_ref=src, dst_ref=dst, send_sem=ss, recv_sem=rs, device_id=dev, device_id_type=MESH)

    inner = lax.div(z * (3 - z), 2)
    flip = lax.div(z, 2)

    def mirrored(b):
        return b + flip * (3 - 2 * b)

    k1, k2, k3 = mirrored(1 - inner), mirrored(2), mirrored(3)

    def plane_of(s):
        return (
            z * lax.div(3 - s, 3)
            + k1 * (lax.rem(s, 2) * lax.div(4 - s, 3))
            + k2 * ((1 - lax.rem(s, 2)) * lax.div(s, 2))
            + k3 * lax.div(s, 3)
        )

    def peer(o):
        return lax.rem(q + o, nq)

    def weight_copies(e, slot):
        return (
            pltpu.make_async_copy(w1_ref.at[e], wb1.at[slot], w_sem.at[slot, 0]),
            pltpu.make_async_copy(w3_ref.at[e], wb3.at[slot], w_sem.at[slot, 1]),
            pltpu.make_async_copy(w2_ref.at[e], wb2.at[slot], w_sem.at[slot, 2]),
        )

    def z_rows(k, dst_z, n):
        return rcopy(xall.at[k], xall.at[k], zs_send.at[n], zs_recv.at[k], at(dst_z, q))

    def z_wait(k):
        rcopy(xall.at[k], xall.at[k], zs_send.at[0], zs_recv.at[k], at(z, q)).wait_recv()
        rcopy(smap.at[k], smap.at[k], sm_send.at[0], sm_recv.at[k], at(z, q)).wait_recv()

    def slot_copy(o):
        dz = lax.rem(z + o, nz)
        return rcopy(slot_ref.at[dz], smap.at[z], sm_send.at[o], sm_recv.at[z], at(dz, q))

    def gate_copy(o):
        d = lax.rem(me + o, ndev)
        return rcopy(sgate_ref.at[d], grecv.at[me], g_send.at[o], g_recv.at[me], at(lax.div(d, nq), lax.rem(d, nq)))

    def d_copy(k, half, o):
        return rcopy(sbuf.at[half, peer(o)], drecv.at[k, q], d_send.at[half, o], d_recv.at[k, q], at(z, peer(o)))

    def r_copy(k, o):
        return rcopy(drecv.at[k, peer(o)], rrecv.at[k, q], r_send.at[k, o], r_recv.at[k, q], at(z, peer(o)))

    def zr_copy(k):
        return rcopy(xall.at[k], zret.at[z], zr_send.at[k], zr_recv.at[z], at(k, q))

    def pack_and_send(s):
        k = plane_of(s)
        half = s % 2
        if s >= 2:
            for o in range(1, nq):
                d_copy(plane_of(s - 2), half, o).wait_send()
        lane_slot = lax.broadcasted_iota(jnp.int32, (cap, tok), 0)
        for d in range(nq):
            hit = lane_slot == smap[k, d : d + 1, :]
            place[k, d * cap : (d + 1) * cap, :] = jnp.where(hit, 1.0, 0.0).astype(BF16)

        @pl.loop(0, hid // nt)
        def _(n):
            cols = pl.ds(pl.multiple_of(n * nt, nt), nt)
            got = jnp.dot(place[k], xall[k, :, cols], preferred_element_type=F32).astype(BF16)
            sbuf[half, :, :, cols] = got.reshape(nq, cap, nt)

        for o in range(1, nq):
            d_copy(k, half, o).start()

        @pl.loop(0, hid // nt)
        def _(n):
            cols = pl.ds(pl.multiple_of(n * nt, nt), nt)
            drecv[k, q, :, cols] = sbuf[half, q, :, cols]

    def d_wait(k):
        for o in range(1, nq):
            r = peer(o)
            rcopy(sbuf.at[0, 0], drecv.at[k, r], d_send.at[0, o], d_recv.at[k, r], at(z, q)).wait_recv()

    def send_back(k):
        for o in range(1, nq):
            r_copy(k, o).start()

        @pl.loop(0, hid // nt)
        def _(n):
            cols = pl.ds(pl.multiple_of(n * nt, nt), nt)
            rrecv[k, q, :, cols] = drecv[k, q, :, cols]

    def r_wait(k):
        for o in range(1, nq):
            r = peer(o)
            rcopy(sbuf.at[0, 0], rrecv.at[k, r], r_send.at[0, o], r_recv.at[k, r], at(z, q)).wait_recv()

    def summed(k, cols):
        got = rrecv[k, :, :, cols].reshape(rows, nt)
        return lax.dot_general(place[k], got, (((0,), (0,)), ((), ())), preferred_element_type=F32)

    def unpack_and_send(k):
        r_wait(k)

        @pl.loop(0, hid // nt)
        def _(n):
            cols = pl.ds(pl.multiple_of(n * nt, nt), nt)
            xall[k, :, cols] = summed(k, cols).astype(BF16)

        zr_copy(k).start()

    for c in weight_copies(0, 0):
        c.start()
    load_x = pltpu.make_async_copy(x_ref, xall.at[z], x_sem)
    load_x.start()
    for o in range(1, nz):
        slot_copy(o).start()
    load_x.wait()

    @pl.when(z > 0)
    def _():
        z_rows(z, z - 1, 0).start()

    @pl.when(z < nz - 1)
    def _():
        z_rows(z, z + 1, 1).start()

    for o in range(1, ndev):
        gate_copy(o).start()
    smap[z] = slot_ref[z]
    grecv[me] = sgate_ref[me]
    pack_and_send(0)

    z_wait(k1)

    @pl.when(inner == 1)
    def _():
        z_wait(k2)
        z_rows(k1, k2, 2).start()
        z_rows(k2, k1, 3).start()

    pack_and_send(1)
    for o in range(1, ndev):
        s = lax.rem(me + o, ndev)
        rcopy(sgate_ref.at[0], grecv.at[s], g_send.at[o], g_recv.at[s], at(z, q)).wait_recv()

    def expert_step(i, _):
        s, e, slot = lax.div(i, 4), lax.rem(i, 4), lax.rem(i, 2)
        k = plane_of(s)

        @pl.when(i < 15)
        def _():
            for c in weight_copies(lax.rem(i + 1, 4), 1 - slot):
                c.start()

        @pl.when(i == 3)
        def _():
            @pl.when(inner == 0)
            def _():
                z_wait(k2)

            @pl.when(inner == 1)
            def _():
                z_wait(k3)
                z_rows(k3, k1, 4).start()

            pack_and_send(2)

        @pl.when(i == 7)
        def _():
            @pl.when(inner == 0)
            def _():
                z_wait(k3)

            pack_and_send(3)

        @pl.when(i == 8)
        def _():
            send_back(k1)

        @pl.when(i == 12)
        def _():
            send_back(k2)

        @pl.when(i == 14)
        def _():
            @pl.when(inner == 1)
            def _():
                z_rows(k1, k2, 2).wait_send()
                z_rows(k2, k1, 3).wait_send()
                z_rows(k3, k1, 4).wait_send()

            unpack_and_send(k1)

        @pl.when(e == 0)
        def _():
            d_wait(k)
            by_slot = grecv[pl.ds(k * nq, nq)].reshape(nq * 8, 128).T
            for r in range(nq):
                for j in range(4):
                    col = by_slot[0:cap, r * 8 + j : r * 8 + j + 1]
                    gb[j, r * cap : (r + 1) * cap, :] = jnp.broadcast_to(col, (cap, 128))

        for c in weight_copies(e, slot):
            c.wait()

        @pl.loop(0, ff // ft)
        def _(n):
            cols = pl.ds(pl.multiple_of(n * ft, ft), ft)
            xin = drecv[k].reshape(rows, hid)
            a = jnp.dot(xin, wb1[slot, :, cols], preferred_element_type=F32)
            b = jnp.dot(xin, wb3[slot, :, cols], preferred_element_type=F32)
            hbuf[:, cols] = (a * jax.nn.sigmoid(a) * b).astype(BF16)

        @pl.loop(0, hid // nt)
        def _(n):
            cols = pl.ds(pl.multiple_of(n * nt, nt), nt)
            o = jnp.dot(hbuf[...], wb2[slot, :, cols], preferred_element_type=F32)
            g = jnp.concatenate([gb[e]] * (nt // 128), axis=1)
            term = jnp.where(g > 0.0, o * g, 0.0)
            acc[:, cols] = jnp.where(e == 0, 0.0, acc[:, cols]) + term

        @pl.when(e == 3)
        def _():
            @pl.loop(0, hid // nt)
            def _(n):
                cols = pl.ds(pl.multiple_of(n * nt, nt), nt)
                drecv[k, :, :, cols] = acc[:, cols].astype(BF16).reshape(nq, cap, nt)

        return 0

    lax.fori_loop(0, 16, expert_step, 0)
    send_back(k3)
    send_back(z)
    unpack_and_send(k2)
    unpack_and_send(k3)
    r_wait(z)
    for o in range(1, nz):
        k = lax.rem(z + o, nz)
        rcopy(xall.at[k], zret.at[k], zr_send.at[0], zr_recv.at[k], at(z, q)).wait_recv()

    @pl.loop(0, hid // nt)
    def _(n):
        cols = pl.ds(pl.multiple_of(n * nt, nt), nt)
        total = summed(z, cols) + xall[z, :, cols].astype(F32)
        for o in range(1, nz):
            total = total + zret[lax.rem(z + o, nz), :, cols].astype(F32)
        out_ref[:, cols] = total.astype(BF16)

    @pl.when(z > 0)
    def _():
        z_rows(z, z - 1, 0).wait_send()

    @pl.when(z < nz - 1)
    def _():
        z_rows(z, z + 1, 1).wait_send()

    for o in range(1, nz):
        slot_copy(o).wait_send()
        zr_copy(lax.rem(z + o, nz)).wait_send()
    for o in range(1, ndev):
        gate_copy(o).wait_send()
    for o in range(1, nq):
        d_copy(k2, 0, o).wait_send()
        d_copy(k3, 1, o).wait_send()
        for s in range(4):
            r_copy(plane_of(s), o).wait_send()


def moe_call(dims, x, slots, slot_gates, w1, w3, w2, capacity):
    nz, ny, nx = dims
    nq = ny * nx
    ndev = nz * nq
    tok, hid = x.shape
    ff = w1.shape[2]
    dma = pltpu.SemaphoreType.DMA
    vmem = pl.BlockSpec(memory_space=pltpu.VMEM)
    hbm = pl.BlockSpec(memory_space=pl.ANY)
    return pl.pallas_call(
        functools.partial(moe_kernel, dims),
        out_shape=jax.ShapeDtypeStruct((tok, hid), BF16),
        in_specs=[hbm, vmem, vmem, hbm, hbm, hbm],
        out_specs=vmem,
        scratch_shapes=[
            pltpu.VMEM((nz, tok, hid), BF16),
            pltpu.VMEM((nz, nq, tok), jnp.int32),
            pltpu.VMEM((ndev, 8, 128), F32),
            pltpu.VMEM((nz, nq * capacity, tok), BF16),
            pltpu.VMEM((2, nq, capacity, hid), BF16),
            pltpu.VMEM((nz, nq, capacity, hid), BF16),
            pltpu.VMEM((nz, nq, capacity, hid), BF16),
            pltpu.VMEM((nz, tok, hid), BF16),
            pltpu.VMEM((nq * capacity, hid), F32),
            pltpu.VMEM((nq * capacity, ff), BF16),
            pltpu.VMEM((4, nq * capacity, 128), F32),
            pltpu.VMEM((2, hid, ff), BF16),
            pltpu.VMEM((2, hid, ff), BF16),
            pltpu.VMEM((2, ff, hid), BF16),
            dma,
            dma((2, 3)),
            dma((5,)),
            dma((nz,)),
            dma((nz,)),
            dma((nz,)),
            dma((ndev,)),
            dma((ndev,)),
            dma((2, nq)),
            dma((nz, nq)),
            dma((nz, nq)),
            dma((nz, nq)),
            dma((nz,)),
            dma((nz,)),
        ],
        compiler_params=pltpu.CompilerParams(has_side_effects=True, vmem_limit_bytes=66 * 1000 * 1000),
    )(x, slots, slot_gates, w1, w3, w2)


def solution(mesh):
    ep_axes = tuple(mesh.axis_names)
    dims = tuple(mesh.shape[axis_name] for axis_name in ep_axes)
    num_devices = math.prod(dims)
    row_spec = P(ep_axes, None)
    w_spec = P(ep_axes, None, None)

    def local_layer(tokens, expert_ids, gate_weights, w_gate, w_up, w_down):
        tok_dev = tokens.shape[0]
        top_k = expert_ids.shape[1]
        local_experts = w_gate.shape[0]
        capacity = tok_dev * top_k // num_devices
        slots, slot_gates = routing_tables(expert_ids, gate_weights, num_devices, local_experts, capacity)
        slots = slots.reshape(dims[0], num_devices // dims[0], tok_dev)
        slot_gates = jnp.pad(slot_gates, ((0, 0), (0, 8 - local_experts), (0, 128 - capacity)))
        return moe_call(dims, tokens, slots, slot_gates, w_gate, w_up, w_down, capacity)

    return jax.shard_map(local_layer, mesh=mesh, in_specs=(row_spec, row_spec, row_spec, w_spec, w_spec, w_spec), out_specs=row_spec, check_vma=False)
```

time: 506 us -> 274 us (0.54)
  Pallas kernels: 0 us -> 262 us
  blocking collectives: 198 us -> 0 us
  waiting for transfers between devices: 109 us -> 0 us
  local copies, waits for them, and re-layouts: 88.3 us -> 4.94 us
  matrix products: 48.8 us -> 0 us
  other arithmetic: 47.4 us -> 4.92 us
  starting transfers between devices: 13 us -> 0 us
    pallas_call x0 -> x1, Pallas kernels: none -> 262 us  [moe_call(): pl.pallas_call(functools.partial(moe_kernel, dims), out_shape=jax.ShapeDt...]
    all_to_all x1 -> x0, blocking collectives: 198 us -> none  [local_layer(): returned = lax.all_to_all(back_rows, ep_axes, 0, 0, tiled=True)]
    all_to_all x2 -> x0, waiting for transfers between devices: 109 us -> none  [the longest x1 109 us: local_layer(): recv_rows = lax.all_to_all(send_rows, ep_axes, 0, 0, tiled=True)]
    dot_general x4 -> x0, matrix products: 48.8 us -> none  [the longest x1 24.3 us: expert_ffn(): jnp.einsum('lcf,lfh->lch', hidden_act, w_down, preferred_element_type=jnp...]
    scatter-add x1 -> x0, other arithmetic: 34.1 us -> none  [local_layer(): jax.ops.segment_sum(weighted.reshape(-1, hidden), pick_rows.reshape(-1),...]
    another operation x3 -> x1, local copies, waits for them, and re-layouts: 30.8 us -> 0.01 us  [the longest x1 30.6 us: local_layer(): jax.ops.segment_sum(weighted.reshape(-1, hidden), pick_rows.reshape(-1),...]
    unnamed x15 -> x3, local copies, waits for them, and re-layouts: 33.9 us -> 3.94 us
    gather x1 -> x0, local copies, waits for them, and re-layouts: 20.8 us -> none  [local_layer(): flat_rows[pick_rows]]
  transfers between devices with their start and end apart: 2 -> 0, of which waited for: 2 -> 0; matrix products, arithmetic and copies ran while one was open for 15% -> 0% of each run, Pallas kernels for 0% -> 0%
where the time goes in v1:
time: 274 us; the launch traced here: 272 us
  Pallas kernels  262 us (96%)
  local copies, waits for them, and re-layouts  4.94 us (2%)
  other arithmetic  4.92 us (2%)
    pallas_call x1, Pallas kernels, moe_call(): pl.pallas_call(functools.partial(moe_kernel, dims), out_shape=jax.ShapeDt...  262 us

profile of v1, /device:TPU:0, one launch (start us, length us, event | category | flops | bytes accessed | tf_op | source)
XLA Modules:
  0.0 272.0 jit_solution(13438990778436441576)
XLA Ops:
  0.0 0.7 add_select_fusion
  0.8 0.6 reduce-window.6
  1.4 0.2 slice_reduce_fusion
  1.6 0.1 fusion.2
  1.7 0.7 fusion.1.slot_ref
  2.4 0.8 copy.21
  3.2 0.8 copy.20
  4.0 1.3 select_reduce_fusion.1
  5.3 0.1 copy.22
  5.4 0.3 iota_compare_fusion
  5.7 1.2 select_reduce_fusion
  6.9 0.7 pad.4.sgate_ref
  7.6 262.0 %shard_map.64 = bf16[256,2048]{1,0:T(8,128)(2,1)} custom-call(bf16[256,2048]{1,0:T(8,128)(2,1)} %x_ref.1, s32[4,8,256]{2,1,0:T(8,128)} %fusion.1.slot_ref, f32[32,8,128]{2,1,0:T(8,128)} %pad.4.sgate_ref, bf16[4,2048,768]{2,1,0:T(8,128)(2,1)} %w1_ref.1, bf16[4,2048,768]{2,1,0:T(8,128)(2,1)} %w3_ref.1, bf16[4,768,2048]{2,1,0:T(8,128)(2,1)} %w2_ref.1), custom_call_target="tpu_custom_call" | custom-call | tf_op jit(solution)/shard_map/pallas_call | solution.py:327
  269.7 2.3 copy.29
  (5 shorter events, 0.1 us)

commit v2 on v1

v2 whole, which is shorter than its diff:
```python
import functools
import math

import jax
import jax.numpy as jnp
from jax import lax
from jax.experimental import pallas as pl
from jax.experimental.pallas import tpu as pltpu
from jax.sharding import PartitionSpec as P

MESH = pl.DeviceIdType.MESH
F32 = jnp.float32
BF16 = jnp.bfloat16


def routing_tables(expert_ids, gate_weights, num_devices, local_experts, capacity):
    tok_dev = expert_ids.shape[0]
    dev_hit = jnp.any((expert_ids // local_experts)[:, :, None] == jnp.arange(num_devices)[None, None, :], axis=1)
    slot_pos = jnp.where(dev_hit, jnp.cumsum(dev_hit.astype(jnp.int32), axis=0) - 1, -1)
    all_experts = jnp.arange(num_devices * local_experts)
    gate_dense = jnp.sum(jnp.where(expert_ids[:, :, None] == all_experts[None, None, :], gate_weights[:, :, None], 0.0), axis=1)
    gate_dense = gate_dense.reshape(tok_dev, num_devices, local_experts)
    place = slot_pos[:, :, None] == jnp.arange(capacity)[None, None, :]
    slot_gates = jnp.sum(jnp.where(place[:, :, None, :], gate_dense[:, :, :, None], 0.0), axis=0)
    return slot_pos.T, slot_gates


ORDER = (
    "p00", "p01", "Y00", "X00", "p10", "X01", "Y01", "p11", "X11", "Y10", "c00", "X10", "p20", "Y20", "c01", "p21",
    "X20", "X21", "Y11", "c02", "c03", "p30", "Y21", "c10", "c11", "X30", "Y30", "c12", "p31", "c13", "y10", "X31",
    "x11", "c20", "c21", "Y31", "c22", "x10", "c23", "y11", "c30", "x21", "c31", "u11", "y21", "c32", "c33", "y31",
    "x31", "y30", "y01", "x30", "u10", "x20", "x01", "u21", "u31", "u30", "y20", "x00", "u20", "u01", "y00", "u00",
)


def moe_kernel(
    dims, x_ref, slot_ref, sgate_ref, w1_ref, w3_ref, w2_ref, out_ref,
    xall, smap, grecv, place, sbuf, drecv, rrecv, zret, acc, hbuf, gb, wb1, wb3, wb2,
    x_sem, w_sem, zs_send, zs_recv, sm_send, sm_recv, g_send, g_recv, d_send, d_recv, r_send, r_recv, zr_send, zr_recv,
):
    nz, ny, nx = dims
    nq = ny * nx
    ndev = nz * nq
    tok, hid = xall.shape[1:]
    cap = sbuf.shape[2]
    ff = wb1.shape[2]
    rows = nq * cap
    nt = 256
    ft = 256
    half = hid // 2
    z = lax.axis_index("ez")
    iy, ix = lax.axis_index("ey"), lax.axis_index("ex")
    q = iy * nx + ix
    me = z * nq + q
    col, core = lax.div(ix, 2), lax.rem(ix, 2)

    def at(zz, qq):
        return (zz, lax.div(qq, nx), lax.rem(qq, nx))

    def rcopy(src, dst, ss, rs, dev):
        return pltpu.make_async_remote_copy(src_ref=src, dst_ref=dst, send_sem=ss, recv_sem=rs, device_id=dev, device_id_type=MESH)

    inner = lax.div(z * (3 - z), 2)
    flip = lax.div(z, 2)

    def mirrored(b):
        return b + flip * (3 - 2 * b)

    k1, k2, k3 = mirrored(1 - inner), mirrored(2), mirrored(3)
    chunk = (z, k1, k2, k3)

    def plane_of(s):
        return (
            z * lax.div(3 - s, 3)
            + k1 * (lax.rem(s, 2) * lax.div(4 - s, 3))
            + k2 * ((1 - lax.rem(s, 2)) * lax.div(s, 2))
            + k3 * lax.div(s, 3)
        )

    def peer(f):
        fy, fx, fc = f // 4, (f // 2) % 2, f % 2
        return (iy + fy * (1 - 2 * iy)) * nx + (col + fx * (1 - 2 * col)) * 2 + core + fc * (1 - 2 * core)

    def hcols(h):
        return pl.ds(h * half, half)

    def tiles(h, body):
        @pl.loop(0, half // nt)
        def _(n):
            body(pl.ds(pl.multiple_of(h * half + n * nt, nt), nt))

    def weight_copies(e, slot):
        return (
            pltpu.make_async_copy(w1_ref.at[e], wb1.at[slot], w_sem.at[slot, 0]),
            pltpu.make_async_copy(w3_ref.at[e], wb3.at[slot], w_sem.at[slot, 1]),
            pltpu.make_async_copy(w2_ref.at[e], wb2.at[slot], w_sem.at[slot, 2]),
        )

    def z_rows(k, dst_z, n, h):
        ref = xall.at[k, :, hcols(h)]
        return rcopy(ref, ref, zs_send.at[n, h], zs_recv.at[k, h], at(dst_z, q))

    def z_wait(k, h):
        z_rows(k, z, 0, h).wait_recv()
        if h == 0:
            rcopy(smap.at[k], smap.at[k], sm_send.at[0], sm_recv.at[k], at(z, q)).wait_recv()

    def slot_copy(o):
        dz = lax.rem(z + o, nz)
        return rcopy(slot_ref.at[dz], smap.at[z], sm_send.at[o], sm_recv.at[z], at(dz, q))

    def gate_copy(o):
        d = lax.rem(me + o, ndev)
        return rcopy(sgate_ref.at[d], grecv.at[me], g_send.at[o], g_recv.at[me], at(lax.div(d, nq), lax.rem(d, nq)))

    def d_copy(s, h, f):
        k = chunk[s]
        return rcopy(sbuf.at[s % 2, peer(f), :, hcols(h)], drecv.at[k, q, :, hcols(h)], d_send.at[2 * (s % 2) + h, f], d_recv.at[2 * k + h, q], at(z, peer(f)))

    def r_copy(s, h, f):
        k = chunk[s]
        return rcopy(drecv.at[k, peer(f), :, hcols(h)], rrecv.at[k, q, :, hcols(h)], r_send.at[2 * s + h, f], r_recv.at[2 * k + h, q], at(z, peer(f)))

    def zr_copy(k, h, n, slot, dst_z):
        return rcopy(xall.at[k, :, hcols(h)], zret.at[slot, :, hcols(h)], zr_send.at[n, h], zr_recv.at[slot, h], at(dst_z, q))

    def zr_wait(slot, h):
        zr_copy(slot, h, 0, slot, z).wait_recv()

    def summed(k, cols):
        got = rrecv[k, :, :, cols].reshape(rows, nt)
        return lax.dot_general(place[k], got, (((0,), (0,)), ((), ())), preferred_element_type=F32)

    def pick(s, h):
        k = chunk[s]
        if s >= 1:
            if s == 1:
                z_wait(k1, h)

            @pl.when(inner == 1)
            def _():
                if s == 1:
                    z_wait(k2, h)
                    z_rows(k1, k2, 2, h).start()
                    z_rows(k2, k1, 3, h).start()
                if s == 2:
                    z_wait(k3, h)
                    z_rows(k3, k1, 4, h).start()

            if s >= 2:
                @pl.when(inner == 0)
                def _():
                    z_wait(k, h)
        if s >= 2:
            for f in range(1, nq):
                d_copy(s - 2, h, f).wait_send()
        if h == 0:
            lane_slot = lax.broadcasted_iota(jnp.int32, (cap, tok), 0)
            for d in range(nq):
                hit = lane_slot == smap[k, d : d + 1, :]
                place[k, d * cap : (d + 1) * cap, :] = jnp.where(hit, 1.0, 0.0).astype(BF16)

        def tile(cols):
            got = jnp.dot(place[k], xall[k, :, cols], preferred_element_type=F32).astype(BF16)
            sbuf[s % 2, :, :, cols] = got.reshape(nq, cap, nt)
            drecv[k, q, :, cols] = sbuf[s % 2, q, :, cols]

        tiles(h, tile)

    def send_picked(s, h, fs):
        for f in fs:
            d_copy(s, h, f).start()

    def d_wait(k):
        for f in range(1, nq):
            r = peer(f)
            for h in range(2):
                blk = drecv.at[k, r, :, hcols(h)]
                rcopy(blk, blk, d_send.at[0, f], d_recv.at[2 * k + h, r], at(z, q)).wait_recv()

    def send_back(s, h, fs):
        for f in fs:
            r_copy(s, h, f).start()
        if 1 in fs:
            def tile(cols):
                rrecv[chunk[s], q, :, cols] = drecv[chunk[s], q, :, cols]

            tiles(h, tile)

    def r_wait(k, h):
        for f in range(1, nq):
            r = peer(f)
            blk = rrecv.at[k, r, :, hcols(h)]
            rcopy(blk, blk, r_send.at[0, f], r_recv.at[2 * k + h, r], at(z, q)).wait_recv()

    def pass_on(s, h):
        k = chunk[s]
        r_wait(k, h)
        if s == 0:
            zr_wait(k1, h)
            zr_wait(k2, h)

            def tile(cols):
                total = summed(k, cols) + xall[k, :, cols].astype(F32)
                total = total + zret[k1, :, cols].astype(F32) + zret[k2, :, cols].astype(F32)
                out_ref[:, cols] = total.astype(BF16)

            tiles(h, tile)
            return

        @pl.when(inner == 1)
        def _():
            n, dst = ((2, k2), (3, k1), (4, k1))[s - 1]
            z_rows(k, dst, n, h).wait_send()

        def plain(cols):
            xall[k, :, cols] = summed(k, cols).astype(BF16)

        if s == 1:
            tiles(h, plain)
        else:
            slot = z if s == 2 else k

            @pl.when(inner == 1)
            def _():
                zr_wait(slot, h)

                def joined(cols):
                    xall[k, :, cols] = (summed(k, cols) + zret[slot, :, cols].astype(F32)).astype(BF16)

                tiles(h, joined)

            @pl.when(inner == 0)
            def _():
                tiles(h, plain)

        if s == 1:
            zr_copy(k, h, s, z, k).start()
        else:
            pl.when(inner == 1)(zr_copy(k, h, s, z, k).start)
            pl.when(inner == 0)(zr_copy(k, h, s, k1 if s == 2 else k, k1).start)

    def run(word):
        what, s, h = word[0], int(word[1]), int(word[2])
        if what == "p":
            pick(s, h)
        if what == "X":
            send_picked(s, h, (1, 2, 3, 6, 7))
        if what == "Y":
            send_picked(s, h, (4, 5))
        if what == "x":
            send_back(s, h, (1, 2, 3, 6, 7))
        if what == "y":
            send_back(s, h, (4, 5))
        if what == "u":
            pass_on(s, h)

    before, seen = {}, 0
    for word in ORDER:
        if word[0] == "c":
            seen += 1
        else:
            before.setdefault(seen, []).append(word)

    load_x = pltpu.make_async_copy(x_ref, xall.at[z], x_sem)
    load_x.start()
    for o in range(1, nz):
        slot_copy(o).start()
    for c in weight_copies(0, 0):
        c.start()
    load_x.wait()
    for h in range(2):
        @pl.when(z > 0)
        def _():
            z_rows(z, z - 1, 0, h).start()

        @pl.when(z < nz - 1)
        def _():
            z_rows(z, z + 1, 1, h).start()

    smap[z] = slot_ref[z]
    for word in before.get(0, ()):
        run(word)
        if word == "X00":
            for o in range(1, ndev):
                gate_copy(o).start()
            grecv[me] = sgate_ref[me]
    for o in range(1, ndev):
        s = lax.rem(me + o, ndev)
        rcopy(sgate_ref.at[0], grecv.at[s], g_send.at[o], g_recv.at[s], at(z, q)).wait_recv()

    def expert_step(i, _):
        s, e, slot = lax.div(i, 4), lax.rem(i, 4), lax.rem(i, 2)
        k = plane_of(s)

        for n in range(1, 16):
            if n in before:
                @pl.when(i == n)
                def _():
                    for word in before[n]:
                        run(word)

        @pl.when(i < 15)
        def _():
            for c in weight_copies(lax.rem(i + 1, 4), 1 - slot):
                c.start()

        @pl.when(e == 0)
        def _():
            d_wait(k)
            by_slot = grecv[pl.ds(k * nq, nq)].reshape(nq * 8, 128).T
            for r in range(nq):
                for j in range(4):
                    one = by_slot[0:cap, r * 8 + j : r * 8 + j + 1]
                    gb[j, r * cap : (r + 1) * cap, :] = jnp.broadcast_to(one, (cap, 128))

        for c in weight_copies(e, slot):
            c.wait()

        @pl.loop(0, ff // ft)
        def _(n):
            cols = pl.ds(pl.multiple_of(n * ft, ft), ft)
            xin = drecv[k].reshape(rows, hid)
            a = jnp.dot(xin, wb1[slot, :, cols], preferred_element_type=F32)
            b = jnp.dot(xin, wb3[slot, :, cols], preferred_element_type=F32)
            hbuf[:, cols] = (a * jax.nn.sigmoid(a) * b).astype(BF16)

        @pl.loop(0, hid // nt)
        def _(n):
            cols = pl.ds(pl.multiple_of(n * nt, nt), nt)
            o = jnp.dot(hbuf[...], wb2[slot, :, cols], preferred_element_type=F32)
            g = jnp.concatenate([gb[e]] * (nt // 128), axis=1)
            term = jnp.where(g > 0.0, o * g, 0.0)
            acc[:, cols] = jnp.where(e == 0, 0.0, acc[:, cols]) + term

        @pl.when(e == 3)
        def _():
            @pl.loop(0, hid // nt)
            def _(n):
                cols = pl.ds(pl.multiple_of(n * nt, nt), nt)
                drecv[k, :, :, cols] = acc[:, cols].astype(BF16).reshape(nq, cap, nt)

        return 0

    lax.fori_loop(0, 16, expert_step, 0)
    for word in before.get(16, ()):
        run(word)

    for h in range(2):
        @pl.when(z > 0)
        def _():
            z_rows(z, z - 1, 0, h).wait_send()

        @pl.when(z < nz - 1)
        def _():
            z_rows(z, z + 1, 1, h).wait_send()

        for s in range(1, 4):
            zr_copy(chunk[s], h, s, z, k1).wait_send()
        for f in range(1, nq):
            for s in range(4):
                r_copy(s, h, f).wait_send()
                if s >= 2:
                    d_copy(s, h, f).wait_send()
    for o in range(1, nz):
        slot_copy(o).wait_send()
    for o in range(1, ndev):
        gate_copy(o).wait_send()


def moe_call(dims, x, slots, slot_gates, w1, w3, w2, capacity):
    nz, ny, nx = dims
    nq = ny * nx
    ndev = nz * nq
    tok, hid = x.shape
    ff = w1.shape[2]
    dma = pltpu.SemaphoreType.DMA
    vmem = pl.BlockSpec(memory_space=pltpu.VMEM)
    hbm = pl.BlockSpec(memory_space=pl.ANY)
    return pl.pallas_call(
        functools.partial(moe_kernel, dims),
        out_shape=jax.ShapeDtypeStruct((tok, hid), BF16),
        in_specs=[hbm, vmem, vmem, hbm, hbm, hbm],
        out_specs=vmem,
        scratch_shapes=[
            pltpu.VMEM((nz, tok, hid), BF16),
            pltpu.VMEM((nz, nq, tok), jnp.int32),
            pltpu.VMEM((ndev, 8, 128), F32),
            pltpu.VMEM((nz, nq * capacity, tok), BF16),
            pltpu.VMEM((2, nq, capacity, hid), BF16),
            pltpu.VMEM((nz, nq, capacity, hid), BF16),
            pltpu.VMEM((nz, nq, capacity, hid), BF16),
            pltpu.VMEM((nz, tok, hid), BF16),
            pltpu.VMEM((nq * capacity, hid), F32),
            pltpu.VMEM((nq * capacity, ff), BF16),
            pltpu.VMEM((4, nq * capacity, 128), F32),
            pltpu.VMEM((2, hid, ff), BF16),
            pltpu.VMEM((2, hid, ff), BF16),
            pltpu.VMEM((2, ff, hid), BF16),
            dma,
            dma((2, 3)),
            dma((5, 2)),
            dma((nz, 2)),
            dma((nz,)),
            dma((nz,)),
            dma((ndev,)),
            dma((ndev,)),
            dma((4, nq)),
            dma((2 * nz, nq)),
            dma((2 * nz, nq)),
            dma((2 * nz, nq)),
            dma((nz, 2)),
            dma((nz, 2)),
        ],
        compiler_params=pltpu.CompilerParams(has_side_effects=True, vmem_limit_bytes=66 * 1000 * 1000),
    )(x, slots, slot_gates, w1, w3, w2)


def solution(mesh):
    ep_axes = tuple(mesh.axis_names)
    dims = tuple(mesh.shape[axis_name] for axis_name in ep_axes)
    num_devices = math.prod(dims)
    row_spec = P(ep_axes, None)
    w_spec = P(ep_axes, None, None)

    def local_layer(tokens, expert_ids, gate_weights, w_gate, w_up, w_down):
        tok_dev = tokens.shape[0]
        top_k = expert_ids.shape[1]
        local_experts = w_gate.shape[0]
        capacity = tok_dev * top_k // num_devices
        slots, slot_gates = routing_tables(expert_ids, gate_weights, num_devices, local_experts, capacity)
        slots = slots.reshape(dims[0], num_devices // dims[0], tok_dev)
        slot_gates = jnp.pad(slot_gates, ((0, 0), (0, 8 - local_experts), (0, 128 - capacity)))
        return moe_call(dims, tokens, slots, slot_gates, w_gate, w_up, w_down, capacity)

    return jax.shard_map(local_layer, mesh=mesh, in_specs=(row_spec, row_spec, row_spec, w_spec, w_spec, w_spec), out_specs=row_spec, check_vma=False)
```

time: 274 us -> 252 us (0.920)
  the two profiles are of different devices: /device:TPU:0 before, /device:TPU:9 now
where the time goes in v2:
time: 252 us
  Pallas kernels  242 us (96%)
  local copies, waits for them, and re-layouts  4.94 us (2%)
  other arithmetic  4.92 us (2%)
    pallas_call x1, Pallas kernels, moe_call(): pl.pallas_call(functools.partial(moe_kernel, dims), out_shape=jax.ShapeDt...  242 us

profile of v2, /device:TPU:9, one launch (start us, length us, event | category | flops | bytes accessed | tf_op | source)
XLA Modules:
  0.0 251.8 jit_solution(15045667047703565617)
XLA Ops:
  0.0 0.7 add_select_fusion
  0.8 0.6 reduce-window.6
  1.4 0.2 slice_reduce_fusion
  1.6 0.1 fusion.2
  1.7 0.7 fusion.1.slot_ref
  2.4 0.8 copy.21
  3.2 0.8 copy.20
  4.0 1.3 select_reduce_fusion.1
  5.3 0.1 copy.22
  5.4 0.3 iota_compare_fusion
  5.7 1.2 select_reduce_fusion
  6.9 0.7 pad.4.sgate_ref
  7.6 241.9 %shard_map.64 = bf16[256,2048]{1,0:T(8,128)(2,1)} custom-call(bf16[256,2048]{1,0:T(8,128)(2,1)} %x_ref.1, s32[4,8,256]{2,1,0:T(8,128)} %fusion.1.slot_ref, f32[32,8,128]{2,1,0:T(8,128)} %pad.4.sgate_ref, bf16[4,2048,768]{2,1,0:T(8,128)(2,1)} %w1_ref.1, bf16[4,2048,768]{2,1,0:T(8,128)(2,1)} %w3_ref.1, bf16[4,768,2048]{2,1,0:T(8,128)(2,1)} %w2_ref.1), custom_call_target="tpu_custom_call" | custom-call | tf_op jit(solution)/shard_map/pallas_call | solution.py:380
  249.5 2.3 copy.29
  (5 shorter events, 0.1 us)

commit v3 on v2

--- a/solution.py
+++ b/solution.py
@@ -13,29 +13,18 @@
 BF16 = jnp.bfloat16
 
 
-def routing_tables(expert_ids, gate_weights, num_devices, local_experts, capacity):
-    tok_dev = expert_ids.shape[0]
-    dev_hit = jnp.any((expert_ids // local_experts)[:, :, None] == jnp.arange(num_devices)[None, None, :], axis=1)
-    slot_pos = jnp.where(dev_hit, jnp.cumsum(dev_hit.astype(jnp.int32), axis=0) - 1, -1)
-    all_experts = jnp.arange(num_devices * local_experts)
-    gate_dense = jnp.sum(jnp.where(expert_ids[:, :, None] == all_experts[None, None, :], gate_weights[:, :, None], 0.0), axis=1)
-    gate_dense = gate_dense.reshape(tok_dev, num_devices, local_experts)
-    place = slot_pos[:, :, None] == jnp.arange(capacity)[None, None, :]
-    slot_gates = jnp.sum(jnp.where(place[:, :, None, :], gate_dense[:, :, :, None], 0.0), axis=0)
-    return slot_pos.T, slot_gates
-
-
 ORDER = (
-    "p00", "p01", "Y00", "X00", "p10", "X01", "Y01", "p11", "X11", "Y10", "c00", "X10", "p20", "Y20", "c01", "p21",
-    "X20", "X21", "Y11", "c02", "c03", "p30", "Y21", "c10", "c11", "X30", "Y30", "c12", "p31", "c13", "y10", "X31",
-    "x11", "c20", "c21", "Y31", "c22", "x10", "c23", "y11", "c30", "x21", "c31", "u11", "y21", "c32", "c33", "y31",
-    "x31", "y30", "y01", "x30", "u10", "x20", "x01", "u21", "u31", "u30", "y20", "x00", "u20", "u01", "y00", "u00",
+    "p00", "p01", "X00", "Y00", "G01", "p10", "G10", "G00", "p11", "X01", "G11", "Y01", "X10", "p20", "X11", "Y20",
+    "c00", "Y10", "Y11", "c01", "X20", "p21", "c02", "G21", "G20", "c03", "c10", "p30", "G30", "c11", "Y21", "X21",
+    "p31", "G31", "c12", "c13", "Y30", "x10", "X31", "y01", "X30", "Y31", "c20", "g10", "c21", "g11", "y10", "c22",
+    "c23", "c30", "c31", "g21", "c32", "x21", "u10", "y21", "c33", "x31", "x30", "g30", "g31", "x20", "y30", "u21",
+    "g20", "y11", "x11", "u30", "x00", "y31", "y20", "g00", "u31", "g01", "u20", "y00", "u11", "x01", "u00", "u01",
 )
 
 
 def moe_kernel(
-    dims, x_ref, slot_ref, sgate_ref, w1_ref, w3_ref, w2_ref, out_ref,
-    xall, smap, grecv, place, sbuf, drecv, rrecv, zret, acc, hbuf, gb, wb1, wb3, wb2,
+    dims, x_ref, ids_ref, gates_ref, w1_ref, w3_ref, w2_ref, out_ref,
+    slot_ref, sgate_ref, dense, xall, smap, grecv, place, sbuf, drecv, rrecv, zret, acc, hbuf, gb, wb1, wb3, wb2,
     x_sem, w_sem, zs_send, zs_recv, sm_send, sm_recv, g_send, g_recv, d_send, d_recv, r_send, r_recv, zr_send, zr_recv,
 ):
     nz, ny, nx = dims
@@ -47,6 +36,7 @@
     rows = nq * cap
     nt = 256
     ft = 256
+    ot = 256
     half = hid // 2
     z = lax.axis_index("ez")
     iy, ix = lax.axis_index("ey"), lax.axis_index("ex")
@@ -240,16 +230,55 @@
             pl.when(inner == 1)(zr_copy(k, h, s, z, k).start)
             pl.when(inner == 0)(zr_copy(k, h, s, k1 if s == 2 else k, k1).start)
 
+    def slot_table():
+        device = lax.broadcasted_iota(jnp.int32, (ndev, tok), 0)
+        hit = None
+        for j in range(ids_ref.shape[0]):
+            here = lax.shift_right_logical(ids_ref[j : j + 1, :], 2) == device
+            hit = here if hit is None else jnp.logical_or(hit, here)
+        hit = jnp.where(hit, 1.0, 0.0)
+        upto = lax.broadcasted_iota(jnp.int32, (tok, tok), 0) <= lax.broadcasted_iota(jnp.int32, (tok, tok), 1)
+        upto = jnp.where(upto, 1.0, 0.0).astype(BF16)
+        count = jnp.dot(hit.astype(BF16), upto, preferred_element_type=F32)
+        slot = jnp.where(hit > 0.0, count - 1.0, -1.0).astype(jnp.int32)
+        slot_ref[...] = slot.reshape(nz, nq, tok)
+
+    def gate_table():
+        row = lax.broadcasted_iota(jnp.int32, (ndev * 8, tok), 0)
+        low = jnp.bitwise_and(row, 7)
+        expert = jnp.where(low < 4, lax.shift_right_logical(row, 3) * 4 + low, -1)
+        gate = jnp.zeros((ndev * 8, tok), F32)
+        for j in range(ids_ref.shape[0]):
+            gate = gate + jnp.where(ids_ref[j : j + 1, :] == expert, gates_ref[j : j + 1, :], 0.0)
+        dense[...] = gate
+
+        @pl.loop(0, ndev, unroll=4)
+        def _(d):
+            g = dense[pl.ds(pl.multiple_of(d * 8, 8), 8), :]
+            hi = g.astype(BF16).astype(F32)
+            mid = (g - hi).astype(BF16).astype(F32)
+            low = g - hi - mid
+            parts = jnp.concatenate([hi, mid, low, jnp.zeros_like(g)], axis=0).astype(BF16)
+            slot = slot_ref[lax.div(d, nq), pl.ds(lax.rem(d, nq), 1), :]
+            spot = lax.broadcasted_iota(jnp.int32, (128, tok), 0) == slot
+            spot = jnp.where(spot, 1.0, 0.0).astype(BF16)
+            got = lax.dot_general(parts, spot, (((1,), (1,)), ((), ())), preferred_element_type=F32)
+            sgate_ref[d] = got[0:8] + got[8:16] + got[16:24]
+
     def run(word):
         what, s, h = word[0], int(word[1]), int(word[2])
         if what == "p":
             pick(s, h)
         if what == "X":
-            send_picked(s, h, (1, 2, 3, 6, 7))
+            send_picked(s, h, (1, 2, 3))
+        if what == "G":
+            send_picked(s, h, (6, 7))
         if what == "Y":
             send_picked(s, h, (4, 5))
         if what == "x":
-            send_back(s, h, (1, 2, 3, 6, 7))
+            send_back(s, h, (1, 2, 3))
+        if what == "g":
+            send_back(s, h, (6, 7))
         if what == "y":
             send_back(s, h, (4, 5))
         if what == "u":
@@ -264,10 +293,11 @@
 
     load_x = pltpu.make_async_copy(x_ref, xall.at[z], x_sem)
     load_x.start()
+    for c in weight_copies(0, 0):
+        c.start()
+    slot_table()
     for o in range(1, nz):
         slot_copy(o).start()
-    for c in weight_copies(0, 0):
-        c.start()
     load_x.wait()
     for h in range(2):
         @pl.when(z > 0)
@@ -279,12 +309,15 @@
             z_rows(z, z + 1, 1, h).start()
 
     smap[z] = slot_ref[z]
+    gates_sent = False
     for word in before.get(0, ()):
-        run(word)
-        if word == "X00":
+        if word[:2] == "p1" and not gates_sent:
+            gates_sent = True
+            gate_table()
             for o in range(1, ndev):
                 gate_copy(o).start()
             grecv[me] = sgate_ref[me]
+        run(word)
     for o in range(1, ndev):
         s = lax.rem(me + o, ndev)
         rcopy(sgate_ref.at[0], grecv.at[s], g_send.at[o], g_recv.at[s], at(z, q)).wait_recv()
@@ -317,7 +350,7 @@
         for c in weight_copies(e, slot):
             c.wait()
 
-        @pl.loop(0, ff // ft)
+        @pl.loop(0, ff // ft, unroll=3)
         def _(n):
             cols = pl.ds(pl.multiple_of(n * ft, ft), ft)
             xin = drecv[k].reshape(rows, hid)
@@ -325,11 +358,11 @@
             b = jnp.dot(xin, wb3[slot, :, cols], preferred_element_type=F32)
             hbuf[:, cols] = (a * jax.nn.sigmoid(a) * b).astype(BF16)
 
-        @pl.loop(0, hid // nt)
+        @pl.loop(0, hid // ot, unroll=8)
         def _(n):
-            cols = pl.ds(pl.multiple_of(n * nt, nt), nt)
+            cols = pl.ds(pl.multiple_of(n * ot, ot), ot)
             o = jnp.dot(hbuf[...], wb2[slot, :, cols], preferred_element_type=F32)
-            g = jnp.concatenate([gb[e]] * (nt // 128), axis=1)
+            g = jnp.concatenate([gb[e]] * (ot // 128), axis=1)
             term = jnp.where(g > 0.0, o * g, 0.0)
             acc[:, cols] = jnp.where(e == 0, 0.0, acc[:, cols]) + term
 
@@ -368,7 +401,7 @@
         gate_copy(o).wait_send()
 
 
-def moe_call(dims, x, slots, slot_gates, w1, w3, w2, capacity):
+def moe_call(dims, x, ids, gates, w1, w3, w2, capacity):
     nz, ny, nx = dims
     nq = ny * nx
     ndev = nz * nq
@@ -383,6 +416,9 @@
         in_specs=[hbm, vmem, vmem, hbm, hbm, hbm],
         out_specs=vmem,
         scratch_shapes=[
+            pltpu.VMEM((nz, nq, tok), jnp.int32),
+            pltpu.VMEM((ndev, 8, 128), F32),
+            pltpu.VMEM((ndev * 8, tok), F32),
             pltpu.VMEM((nz, tok, hid), BF16),
             pltpu.VMEM((nz, nq, tok), jnp.int32),
             pltpu.VMEM((ndev, 8, 128), F32),
@@ -413,7 +449,7 @@
             dma((nz, 2)),
         ],
         compiler_params=pltpu.CompilerParams(has_side_effects=True, vmem_limit_bytes=66 * 1000 * 1000),
-    )(x, slots, slot_gates, w1, w3, w2)
+    )(x, ids, gates, w1, w3, w2)
 
 
 def solution(mesh):
@@ -426,11 +462,7 @@
     def local_layer(tokens, expert_ids, gate_weights, w_gate, w_up, w_down):
         tok_dev = tokens.shape[0]
         top_k = expert_ids.shape[1]
-        local_experts = w_gate.shape[0]
         capacity = tok_dev * top_k // num_devices
-        slots, slot_gates = routing_tables(expert_ids, gate_weights, num_devices, local_experts, capacity)
-        slots = slots.reshape(dims[0], num_devices // dims[0], tok_dev)
-        slot_gates = jnp.pad(slot_gates, ((0, 0), (0, 8 - local_experts), (0, 128 - capacity)))
-        return moe_call(dims, tokens, slots, slot_gates, w_gate, w_up, w_down, capacity)
+        return moe_call(dims, tokens, expert_ids.T, gate_weights.T, w_gate, w_up, w_down, capacity)
 
     return jax.shard_map(local_layer, mesh=mesh, in_specs=(row_spec, row_spec, row_spec, w_spec, w_spec, w_spec), out_specs=row_spec, check_vma=False)

time: 252 us -> 239 us (0.948)
  the two profiles are of different devices: /device:TPU:9 before, /device:TPU:0 now
where the time goes in v3:
time: 239 us; the launch traced here: 234 us
  Pallas kernels  232 us (97%)
    pallas_call x1, Pallas kernels, moe_call(): pl.pallas_call(functools.partial(moe_kernel, dims), out_shape=jax.ShapeDt...  232 us

profile of v3, /device:TPU:0, one launch (start us, length us, event | category | flops | bytes accessed | tf_op | source)
XLA Modules:
  0.0 234.1 jit_solution(14514477429663907898)
XLA Ops:
  0.0 231.8 %shard_map.64 = bf16[256,2048]{1,0:T(8,128)(2,1)} custom-call(bf16[256,2048]{1,0:T(8,128)(2,1)} %x_ref.1, s32[8,256]{1,0:T(8,128)} %bitcast.2, f32[8,256]{1,0:T(8,128)} %bitcast.3, bf16[4,2048,768]{2,1,0:T(8,128)(2,1)} %w1_ref.1, bf16[4,2048,768]{2,1,0:T(8,128)(2,1)} %w3_ref.1, bf16[4,768,2048]{2,1,0:T(8,128)(2,1)} %w2_ref.1), custom_call_target="tpu_custom_call" | custom-call | tf_op jit(solution)/shard_map/pallas_call | solution.py:413
  231.8 2.3 copy.8

commit v4 on v3

--- a/solution.py
+++ b/solution.py
@@ -291,14 +291,21 @@
         else:
             before.setdefault(seen, []).append(word)
 
+    barrier = pltpu.get_barrier_semaphore()
+    for o in range(1, ndev):
+        d = lax.rem(me + o, ndev)
+        pl.semaphore_signal(barrier, inc=1, device_id=at(lax.div(d, nq), lax.rem(d, nq)), device_id_type=MESH)
     load_x = pltpu.make_async_copy(x_ref, xall.at[z], x_sem)
     load_x.start()
     for c in weight_copies(0, 0):
         c.start()
     slot_table()
+    smap[z] = slot_ref[z]
+    load_x.wait()
+    run(ORDER[0])
+    pl.semaphore_wait(barrier, ndev - 1)
     for o in range(1, nz):
         slot_copy(o).start()
-    load_x.wait()
     for h in range(2):
         @pl.when(z > 0)
         def _():
@@ -308,9 +315,8 @@
         def _():
             z_rows(z, z + 1, 1, h).start()
 
-    smap[z] = slot_ref[z]
     gates_sent = False
-    for word in before.get(0, ()):
+    for word in before.get(0, ())[1:]:
         if word[:2] == "p1" and not gates_sent:
             gates_sent = True
             gate_table()
@@ -448,7 +454,7 @@
             dma((nz, 2)),
             dma((nz, 2)),
         ],
-        compiler_params=pltpu.CompilerParams(has_side_effects=True, vmem_limit_bytes=66 * 1000 * 1000),
+        compiler_params=pltpu.CompilerParams(collective_id=0, has_side_effects=True, vmem_limit_bytes=66 * 1000 * 1000),
     )(x, ids, gates, w1, w3, w2)
 
 

time: 239 us -> 227 us (0.950); the launches traced: 234 us -> 227 us
  Pallas kernels: 232 us -> 224 us
    pallas_call x1, Pallas kernels: 232 us -> 224 us  [moe_call(): pl.pallas_call(functools.partial(moe_kernel, dims), out_shape=jax.ShapeDt...]
where the time goes in v4:
time: 227 us
  Pallas kernels  224 us (99%)
  local copies, waits for them, and re-layouts  2.3 us (1%)
    pallas_call x1, Pallas kernels, moe_call(): pl.pallas_call(functools.partial(moe_kernel, dims), out_shape=jax.ShapeDt...  224 us

profile of v4, /device:TPU:0, one launch (start us, length us, event | category | flops | bytes accessed | tf_op | source)
XLA Modules:
  0.0 226.7 jit_solution(7190525662723745492)
XLA Ops:
  0.0 224.4 %shard_map.64 = bf16[256,2048]{1,0:T(8,128)(2,1)} custom-call(bf16[256,2048]{1,0:T(8,128)(2,1)} %x_ref.1, s32[8,256]{1,0:T(8,128)} %bitcast.2, f32[8,256]{1,0:T(8,128)} %bitcast.3, bf16[4,2048,768]{2,1,0:T(8,128)(2,1)} %w1_ref.1, bf16[4,2048,768]{2,1,0:T(8,128)(2,1)} %w3_ref.1, bf16[4,768,2048]{2,1,0:T(8,128)(2,1)} %w2_ref.1), custom_call_target="tpu_custom_call" | custom-call | tf_op jit(solution)/shard_map/pallas_call | solution.py:419
  224.4 2.3 %copy.8 = bf16[256,2048]{1,0:T(8,128)(2,1)} copy(bf16[256,2048]{1,0:T(8,128)(2,1)} %shard_map.64) | data formatting | bytes 2097152

commit v5 on v4

v5 whole, which is shorter than its diff:
```python
import functools
import math

import jax
import jax.numpy as jnp
from jax import lax
from jax.experimental import pallas as pl
from jax.experimental.pallas import tpu as pltpu
from jax.sharding import PartitionSpec as P

MESH = pl.DeviceIdType.MESH
F32 = jnp.float32
BF16 = jnp.bfloat16


ORDER = (
    "e00", "e01", "p00", "p01", "e10", "e11", "c00", "p10", "c01", "e20", "p11", "c02", "c03", "e21", "p20", "c10",
    "e30", "p21", "c11", "c12", "e31", "c13", "b11", "c20", "p31", "c21", "p30", "n11", "c22", "c23", "b10", "b20",
    "c30", "c31", "b21", "c32", "n20", "u11", "c33", "b31", "b30", "u20", "n31", "b00", "n30", "n10", "n21", "u31",
    "u30", "b01", "n00", "u21", "u10", "n01", "u00", "u01",
)
LAST = ((0, 1, 4, 5), (0, 1, 2, 3))
SWAP = (2, 4)


def moe_kernel(
    dims, x_ref, ids_ref, gates_ref, w1_ref, w3_ref, w2_ref, out_ref,
    slot_ref, sgate_ref, dense, xall, xnb, smap, grecv, place, sbuf, drecv, rrecv, prcv, zret, acc, hbuf, gb, wb1, wb3, wb2,
    x_sem, w_sem, zs_send, zs_recv, sm_send, sm_recv, g_send, g_recv, e_send, e_recv, d_send, d_recv, r_send, r_recv,
    p_send, p_recv, zr_send, zr_recv,
):
    nz, ny, nx = dims
    nq = ny * nx
    ndev = nz * nq
    tok, hid = xall.shape[1:]
    cap = sbuf.shape[3]
    ff = wb1.shape[2]
    rows = nq * cap
    nt = 256
    ft = 256
    ot = 256
    quarter = hid // 4
    z = lax.axis_index("ez")
    iy, ix = lax.axis_index("ey"), lax.axis_index("ex")
    q = iy * nx + ix
    me = z * nq + q
    col, core = lax.div(ix, 2), lax.rem(ix, 2)

    def at(zz, qq):
        return (zz, lax.div(qq, nx), lax.rem(qq, nx))

    def rcopy(src, dst, ss, rs, dev):
        return pltpu.make_async_remote_copy(src_ref=src, dst_ref=dst, send_sem=ss, recv_sem=rs, device_id=dev, device_id_type=MESH)

    inner = lax.div(z * (3 - z), 2)
    flip = lax.div(z, 2)

    def mirrored(b):
        return b + flip * (3 - 2 * b)

    k1, k2, k3 = mirrored(1 - inner), mirrored(2), mirrored(3)
    chunk = (z, k1, k2, k3)

    def plane_of(s):
        return (
            z * lax.div(3 - s, 3)
            + k1 * (lax.rem(s, 2) * lax.div(4 - s, 3))
            + k2 * ((1 - lax.rem(s, 2)) * lax.div(s, 2))
            + k3 * lax.div(s, 3)
        )

    def peer(f):
        fy, fx, fc = f // 4, (f // 2) % 2, f % 2
        return (iy + fy * (1 - 2 * iy)) * nx + (col + fx * (1 - 2 * col)) * 2 + core + fc * (1 - 2 * core)

    def part(h, g):
        return pl.ds((2 * g + h) * quarter, quarter)

    def tiles(h, g, body):
        @pl.loop(0, quarter // nt)
        def _(n):
            body(pl.ds(pl.multiple_of((2 * g + h) * quarter + n * nt, nt), nt))

    def weight_copies(e, slot):
        return (
            pltpu.make_async_copy(w1_ref.at[e], wb1.at[slot], w_sem.at[slot, 0]),
            pltpu.make_async_copy(w3_ref.at[e], wb3.at[slot], w_sem.at[slot, 1]),
        )

    def down_copy(e):
        return pltpu.make_async_copy(w2_ref.at[e], wb2, w_sem.at[0, 2])

    def z_rows(k, dst_z, n, h, g):
        ref = xall.at[k, :, part(h, g)]
        return rcopy(ref, ref, zs_send.at[n, h], zs_recv.at[k, h], at(dst_z, q))

    def pair(ref, ss, rs):
        both = ref.at[0, :, pl.ds(0, 2 * quarter)]
        return rcopy(both, both, ss, rs, at(z, q))

    def z_wait(k, h):
        pair(xall, zs_send.at[0, h], zs_recv.at[k, h]).wait_recv()

    def z_sent(n, h):
        pair(xall, zs_send.at[n, h], zs_recv.at[0, h]).wait_send()

    def blocks(n, ss, rs):
        ref = drecv.at[0, pl.ds(0, n), :, pl.ds(0, 2 * quarter)]
        return rcopy(ref, ref, ss, rs, at(z, q))

    def tables(ref, n, ss, rs):
        ref = ref.at[pl.ds(0, n)]
        return rcopy(ref, ref, ss, rs, at(z, q))

    def slot_copy(o, role):
        dz = lax.rem(z + o, nz)
        return rcopy(slot_ref.at[dz], smap.at[z, role], sm_send, sm_recv.at[z], at(dz, peer((0, 2, 4)[role])))

    def gate_copy(o):
        d = lax.rem(me + o, ndev)
        return rcopy(sgate_ref.at[d], grecv.at[me], g_send, g_recv, at(lax.div(d, nq), lax.rem(d, nq)))

    def source(f, g, src):
        return peer(f ^ (SWAP[g] * src))

    def e_copy(s, h, g):
        k = chunk[s]
        return rcopy(xall.at[k, :, part(h, g)], xnb.at[k, :, part(h, g)], e_send.at[s, h], e_recv.at[k, h], at(z, peer(SWAP[g])))

    def d_copy(s, h, g, src, i):
        k = chunk[s]
        to = drecv.at[k, source(0, g, src), :, part(h, g)]
        return rcopy(sbuf.at[s % 2, src, i, :, part(h, g)], to, d_send.at[s % 2, h], d_recv.at[k, h], at(z, peer(LAST[g][i])))

    def r_copy(s, h, g, src, i):
        k, f = chunk[s], LAST[g][i]
        to = rrecv.at[k, src, i, :, part(h, g)]
        return rcopy(drecv.at[k, source(f, g, src), :, part(h, g)], to, r_send.at[s, h], r_recv.at[k, 2 * h + src], at(z, peer(f)))

    def p_copy(s, h, g):
        k = chunk[s]
        return rcopy(xnb.at[k, :, part(h, g)], prcv.at[k, :, part(h, g)], p_send.at[s, h], p_recv.at[k, h], at(z, peer(SWAP[g])))

    def zr_copy(k, h, g, n, slot, dst_z):
        to = zret.at[slot, :, part(h, g)]
        return rcopy(xall.at[k, :, part(h, g)], to, zr_send.at[n, h], zr_recv.at[slot, h], at(dst_z, q))

    def zr_wait(slot, h):
        pair(zret, zr_send.at[0, h], zr_recv.at[slot, h]).wait_recv()

    def summed(k, g, src, cols):
        got = rrecv[k, src, :, :, cols].reshape(4 * cap, nt)
        return lax.dot_general(place[k, 2 * g + src], got, (((0,), (0,)), ((), ())), preferred_element_type=F32)

    def swap_rows(s, h):
        k = chunk[s]
        if s == 1:
            z_wait(k1, h)
        if s >= 1:
            @pl.when(inner == 1)
            def _():
                if s == 1:
                    z_wait(k2, h)
                    for g in range(2):
                        z_rows(k1, k2, 2, h, g).start()
                        z_rows(k2, k1, 3, h, g).start()
                if s == 2:
                    z_wait(k3, h)
                    for g in range(2):
                        z_rows(k3, k1, 4, h, g).start()

        if s >= 2:
            @pl.when(inner == 0)
            def _():
                z_wait(k, h)
        for g in range(2):
            e_copy(s, h, g).start()

    placed = set()

    def pick(s, h):
        k = chunk[s]
        pair(xnb, e_send.at[s, h], e_recv.at[k, h]).wait_recv()
        if s >= 2:
            blocks(6, d_send.at[s % 2, h], d_recv.at[k, h]).wait_send()
        if s not in placed:
            placed.add(s)
            tables(smap.at[k], 3 if s else 2, sm_send, sm_recv.at[k]).wait_recv()
            lane_slot = lax.broadcasted_iota(jnp.int32, (cap, tok), 0)
            for g in range(2):
                for src in range(2):
                    for i in range(4):
                        hit = lane_slot == smap[k, src * (1 + g), pl.ds(peer(LAST[g][i]), 1), :]
                        place[k, 2 * g + src, i * cap : (i + 1) * cap, :] = jnp.where(hit, 1.0, 0.0).astype(BF16)
        for g in range(2):
            for src in range(2):
                rows_of = xnb if src else xall

                def tile(cols, g=g, src=src, rows_of=rows_of):
                    got = jnp.dot(place[k, 2 * g + src], rows_of[k, :, cols], preferred_element_type=F32).astype(BF16)
                    sbuf[s % 2, src, :, :, cols] = got.reshape(4, cap, nt)
                    drecv[k, source(0, g, src), :, cols] = sbuf[s % 2, src, 0, :, cols]

                tiles(h, g, tile)
                for i in range(1, 4):
                    d_copy(s, h, g, src, i).start()

    def d_wait(k):
        for h in range(2):
            blocks(6, d_send.at[0, h], d_recv.at[k, h]).wait_recv()

    def send_back(s, h):
        k = chunk[s]
        for src in (1, 0):
            for i in range(1, 4):
                for g in range(2):
                    r_copy(s, h, g, src, i).start()
        for g in range(2):
            def tile(cols, g=g):
                for src in range(2):
                    rrecv[k, src, 0, :, cols] = drecv[k, source(0, g, src), :, cols]

            tiles(h, g, tile)

    def r_wait(s, h, src):
        k = chunk[s]
        blocks(3, r_send.at[s, h], r_recv.at[k, 2 * h + src]).wait_recv()

    def sum_neighbour(s, h):
        k = chunk[s]
        r_wait(s, h, 1)
        for g in range(2):
            def tile(cols, g=g):
                xnb[k, :, cols] = summed(k, g, 1, cols).astype(BF16)

            tiles(h, g, tile)
            p_copy(s, h, g).start()

    def pass_on(s, h):
        k = chunk[s]
        r_wait(s, h, 0)
        pair(prcv, p_send.at[s, h], p_recv.at[k, h]).wait_recv()

        def own(g, cols):
            return summed(k, g, 0, cols) + prcv[k, :, cols].astype(F32)

        if s == 0:
            zr_wait(k1, h)
            zr_wait(k2, h)
            for g in range(2):
                def tile(cols, g=g):
                    total = own(g, cols) + xall[k, :, cols].astype(F32)
                    total = total + zret[k1, :, cols].astype(F32) + zret[k2, :, cols].astype(F32)
                    out_ref[:, cols] = total.astype(BF16)

                tiles(h, g, tile)
            return

        pair(xall, e_send.at[s, h], e_recv.at[k, h]).wait_send()

        @pl.when(inner == 1)
        def _():
            z_sent(s + 1, h)

        def plain():
            for g in range(2):
                def tile(cols, g=g):
                    xall[k, :, cols] = own(g, cols).astype(BF16)

                tiles(h, g, tile)

        if s == 1:
            plain()
            for g in range(2):
                zr_copy(k, h, g, s, z, k).start()
            return
        slot = z if s == 2 else k

        @pl.when(inner == 1)
        def _():
            zr_wait(slot, h)
            for g in range(2):
                def tile(cols, g=g):
                    xall[k, :, cols] = (own(g, cols) + zret[slot, :, cols].astype(F32)).astype(BF16)

                tiles(h, g, tile)
                zr_copy(k, h, g, s, z, k).start()

        @pl.when(inner == 0)
        def _():
            plain()
            for g in range(2):
                zr_copy(k, h, g, s, k1 if s == 2 else k, k1).start()

    def slot_table():
        device = lax.broadcasted_iota(jnp.int32, (ndev, tok), 0)
        hit = None
        for j in range(ids_ref.shape[0]):
            here = lax.shift_right_logical(ids_ref[j : j + 1, :], 2) == device
            hit = here if hit is None else jnp.logical_or(hit, here)
        hit = jnp.where(hit, 1.0, 0.0)
        upto = lax.broadcasted_iota(jnp.int32, (tok, tok), 0) <= lax.broadcasted_iota(jnp.int32, (tok, tok), 1)
        upto = jnp.where(upto, 1.0, 0.0).astype(BF16)
        count = jnp.dot(hit.astype(BF16), upto, preferred_element_type=F32)
        slot = jnp.where(hit > 0.0, count - 1.0, -1.0).astype(jnp.int32)
        slot_ref[...] = slot.reshape(nz, nq, tok)

    def gate_table():
        row = lax.broadcasted_iota(jnp.int32, (ndev * 8, tok), 0)
        low = jnp.bitwise_and(row, 7)
        expert = jnp.where(low < 4, lax.shift_right_logical(row, 3) * 4 + low, -1)
        gate = jnp.zeros((ndev * 8, tok), F32)
        for j in range(ids_ref.shape[0]):
            gate = gate + jnp.where(ids_ref[j : j + 1, :] == expert, gates_ref[j : j + 1, :], 0.0)
        dense[...] = gate

        @pl.loop(0, ndev, unroll=4)
        def _(d):
            g = dense[pl.ds(pl.multiple_of(d * 8, 8), 8), :]
            hi = g.astype(BF16).astype(F32)
            mid = (g - hi).astype(BF16).astype(F32)
            low = g - hi - mid
            parts = jnp.concatenate([hi, mid, low, jnp.zeros_like(g)], axis=0).astype(BF16)
            slot = slot_ref[lax.div(d, nq), pl.ds(lax.rem(d, nq), 1), :]
            spot = lax.broadcasted_iota(jnp.int32, (128, tok), 0) == slot
            spot = jnp.where(spot, 1.0, 0.0).astype(BF16)
            got = lax.dot_general(parts, spot, (((1,), (1,)), ((), ())), preferred_element_type=F32)
            sgate_ref[d] = got[0:8] + got[8:16] + got[16:24]

    steps = {"e": swap_rows, "p": pick, "b": send_back, "n": sum_neighbour, "u": pass_on}

    def run(word):
        steps[word[0]](int(word[1]), int(word[2]))

    before, seen = {}, 0
    for word in ORDER:
        if word[0] == "c":
            seen += 1
        else:
            before.setdefault(seen, []).append(word)

    barrier = pltpu.get_barrier_semaphore()

    @pl.loop(1, ndev)
    def _(o):
        d = lax.rem(me + o, ndev)
        pl.semaphore_signal(barrier, inc=1, device_id=at(lax.div(d, nq), lax.rem(d, nq)), device_id_type=MESH)

    load_x = pltpu.make_async_copy(x_ref, xall.at[z], x_sem)
    load_x.start()
    for c in weight_copies(0, 0):
        c.start()
    slot_table()
    smap[z, 0] = slot_ref[z]
    load_x.wait()
    pl.semaphore_wait(barrier, ndev - 1)
    for h in range(2):
        for g in range(2):
            @pl.when(z > 0)
            def _():
                z_rows(z, z - 1, 0, h, g).start()

            @pl.when(z < nz - 1)
            def _():
                z_rows(z, z + 1, 1, h, g).start()

        swap_rows(0, h)
        for o in range(nz):
            for role in range(3):
                if h == 0 and (o or role):
                    slot_copy(o, role).start()
    gate_table()

    @pl.loop(1, ndev)
    def _(o):
        gate_copy(o).start()

    grecv[me] = sgate_ref[me]
    for word in before.get(0, ())[2:]:
        run(word)
    tables(grecv, ndev - 1, g_send, g_recv).wait_recv()

    def expert_step(i, _):
        s, e, slot = lax.div(i, 4), lax.rem(i, 4), lax.rem(i, 2)
        k = plane_of(s)

        for n in range(1, 16):
            if n in before:
                @pl.when(i == n)
                def _():
                    for word in before[n]:
                        run(word)

        down_copy(e).start()

        @pl.when(i < 15)
        def _():
            for c in weight_copies(lax.rem(i + 1, 4), 1 - slot):
                c.start()

        @pl.when(e == 0)
        def _():
            d_wait(k)
            by_slot = grecv[pl.ds(k * nq, nq)].reshape(nq * 8, 128).T
            for r in range(nq):
                for j in range(4):
                    one = by_slot[0:cap, r * 8 + j : r * 8 + j + 1]
                    gb[j, r * cap : (r + 1) * cap, :] = jnp.broadcast_to(one, (cap, 128))

        for c in weight_copies(e, slot):
            c.wait()

        @pl.loop(0, ff // ft, unroll=3)
        def _(n):
            cols = pl.ds(pl.multiple_of(n * ft, ft), ft)
            xin = drecv[k].reshape(rows, hid)
            a = jnp.dot(xin, wb1[slot, :, cols], preferred_element_type=F32)
            b = jnp.dot(xin, wb3[slot, :, cols], preferred_element_type=F32)
            hbuf[:, cols] = (a * jax.nn.sigmoid(a) * b).astype(BF16)

        down_copy(e).wait()

        @pl.loop(0, hid // ot, unroll=8)
        def _(n):
            cols = pl.ds(pl.multiple_of(n * ot, ot), ot)
            o = jnp.dot(hbuf[...], wb2[:, cols], preferred_element_type=F32)
            g = jnp.concatenate([gb[e]] * (ot // 128), axis=1)
            term = jnp.where(g > 0.0, o * g, 0.0)
            acc[:, cols] = jnp.where(e == 0, 0.0, acc[:, cols]) + term

        @pl.when(e == 3)
        def _():
            @pl.loop(0, hid // nt)
            def _(n):
                cols = pl.ds(pl.multiple_of(n * nt, nt), nt)
                drecv[k, :, :, cols] = acc[:, cols].astype(BF16).reshape(nq, cap, nt)

        return 0

    lax.fori_loop(0, 16, expert_step, 0)
    for word in before.get(16, ()):
        run(word)

    for h in range(2):
        @pl.when(z > 0)
        def _():
            z_sent(0, h)

        @pl.when(z < nz - 1)
        def _():
            z_sent(1, h)

        pair(xall, e_send.at[0, h], e_recv.at[0, h]).wait_send()
        for s in range(4):
            pair(xnb, p_send.at[s, h], p_recv.at[0, h]).wait_send()
            if s:
                pair(xall, zr_send.at[s, h], zr_recv.at[0, h]).wait_send()
            if s >= 2:
                blocks(6, d_send.at[s % 2, h], d_recv.at[0, h]).wait_send()
            blocks(6, r_send.at[s, h], r_recv.at[0, h]).wait_send()
    tables(sgate_ref, ndev - 1, g_send, g_recv).wait_send()
    tables(sgate_ref, 2 * (3 * nz - 1), sm_send, sm_recv.at[0]).wait_send()


def moe_call(dims, x, ids, gates, w1, w3, w2, capacity):
    nz, ny, nx = dims
    nq = ny * nx
    ndev = nz * nq
    tok, hid = x.shape
    ff = w1.shape[2]
    dma = pltpu.SemaphoreType.DMA
    vmem = pl.BlockSpec(memory_space=pltpu.VMEM)
    hbm = pl.BlockSpec(memory_space=pl.ANY)
    return pl.pallas_call(
        functools.partial(moe_kernel, dims),
        out_shape=jax.ShapeDtypeStruct((tok, hid), BF16),
        in_specs=[hbm, vmem, vmem, hbm, hbm, hbm],
        out_specs=vmem,
        scratch_shapes=[
            pltpu.VMEM((nz, nq, tok), jnp.int32),
            pltpu.VMEM((ndev, 8, 128), F32),
            pltpu.VMEM((ndev * 8, tok), F32),
            pltpu.VMEM((nz, tok, hid), BF16),
            pltpu.VMEM((nz, tok, hid), BF16),
            pltpu.VMEM((nz, 3, nq, tok), jnp.int32),
            pltpu.VMEM((ndev, 8, 128), F32),
            pltpu.VMEM((nz, 4, 4 * capacity, tok), BF16),
            pltpu.VMEM((2, 2, 4, capacity, hid), BF16),
            pltpu.VMEM((nz, nq, capacity, hid), BF16),
            pltpu.VMEM((nz, 2, 4, capacity, hid), BF16),
            pltpu.VMEM((nz, tok, hid), BF16),
            pltpu.VMEM((nz, tok, hid), BF16),
            pltpu.VMEM((nq * capacity, hid), F32),
            pltpu.VMEM((nq * capacity, ff), BF16),
            pltpu.VMEM((4, nq * capacity, 128), F32),
            pltpu.VMEM((2, hid, ff), BF16),
            pltpu.VMEM((2, hid, ff), BF16),
            pltpu.VMEM((ff, hid), BF16),
            dma,
            dma((2, 3)),
            dma((5, 2)),
            dma((nz, 2)),
            dma,
            dma((nz,)),
            dma,
            dma,
            dma((nz, 2)),
            dma((nz, 2)),
            dma((2, 2)),
            dma((nz, 2)),
            dma((nz, 2)),
            dma((nz, 4)),
            dma((nz, 2)),
            dma((nz, 2)),
            dma((nz, 2)),
            dma((nz, 2)),
        ],
        compiler_params=pltpu.CompilerParams(collective_id=0, has_side_effects=True, vmem_limit_bytes=67 * 1000 * 1000),
    )(x, ids, gates, w1, w3, w2)


def solution(mesh):
    ep_axes = tuple(mesh.axis_names)
    dims = tuple(mesh.shape[axis_name] for axis_name in ep_axes)
    num_devices = math.prod(dims)
    row_spec = P(ep_axes, None)
    w_spec = P(ep_axes, None, None)

    def local_layer(tokens, expert_ids, gate_weights, w_gate, w_up, w_down):
        tok_dev = tokens.shape[0]
        top_k = expert_ids.shape[1]
        capacity = tok_dev * top_k // num_devices
        return moe_call(dims, tokens, expert_ids.T, gate_weights.T, w_gate, w_up, w_down, capacity)

    return jax.shard_map(local_layer, mesh=mesh, in_specs=(row_spec, row_spec, row_spec, w_spec, w_spec, w_spec), out_specs=row_spec, check_vma=False)
```

time: 227 us -> 213 us (0.938)
  Pallas kernels: 224 us -> 210 us
    pallas_call x1, Pallas kernels: 224 us -> 210 us  [moe_call(): pl.pallas_call(functools.partial(moe_kernel, dims), out_shape=jax.ShapeDt...]
where the time goes in v5:
time: 213 us
  Pallas kernels  210 us (99%)
  local copies, waits for them, and re-layouts  2.3 us (1%)
    pallas_call x1, Pallas kernels, moe_call(): pl.pallas_call(functools.partial(moe_kernel, dims), out_shape=jax.ShapeDt...  210 us

profile of v5, /device:TPU:0, one launch (start us, length us, event | category | flops | bytes accessed | tf_op | source)
XLA Modules:
  0.0 212.7 jit_solution(13112507061056040076)
XLA Ops:
  0.0 210.4 %shard_map.64 = bf16[256,2048]{1,0:T(8,128)(2,1)} custom-call(bf16[256,2048]{1,0:T(8,128)(2,1)} %x_ref.1, s32[8,256]{1,0:T(8,128)} %bitcast.2, f32[8,256]{1,0:T(8,128)} %bitcast.3, bf16[4,2048,768]{2,1,0:T(8,128)(2,1)} %w1_ref.1, bf16[4,2048,768]{2,1,0:T(8,128)(2,1)} %w3_ref.1, bf16[4,768,2048]{2,1,0:T(8,128)(2,1)} %w2_ref.1), custom_call_target="tpu_custom_call" | custom-call | tf_op jit(solution)/shard_map/pallas_call | solution.py:474
  210.4 2.3 %copy.8 = bf16[256,2048]{1,0:T(8,128)(2,1)} copy(bf16[256,2048]{1,0:T(8,128)(2,1)} %shard_map.64) | data formatting | bytes 2097152

commit v6 on v5

--- a/solution.py
+++ b/solution.py
@@ -14,10 +14,10 @@
 
 
 ORDER = (
-    "e00", "e01", "p00", "p01", "e10", "e11", "c00", "p10", "c01", "e20", "p11", "c02", "c03", "e21", "p20", "c10",
-    "e30", "p21", "c11", "c12", "e31", "c13", "b11", "c20", "p31", "c21", "p30", "n11", "c22", "c23", "b10", "b20",
-    "c30", "c31", "b21", "c32", "n20", "u11", "c33", "b31", "b30", "u20", "n31", "b00", "n30", "n10", "n21", "u31",
-    "u30", "b01", "n00", "u21", "u10", "n01", "u00", "u01",
+    "e00", "e01", "p00", "p01", "e10", "e11", "c00", "p10", "c01", "p11", "e20", "c02", "c03", "e21", "c10", "p20",
+    "c11", "p21", "c12", "e30", "c13", "e31", "c20", "b11", "p30", "c21", "p31", "c22", "n11", "c23", "b20", "b01",
+    "c30", "c31", "u11", "n20", "c32", "c33", "b31", "b30", "u20", "n31", "b21", "n30", "u31", "b10", "n21", "u30",
+    "n10", "b00", "u21", "n01", "u10", "n00", "u01", "u00",
 )
 LAST = ((0, 1, 4, 5), (0, 1, 2, 3))
 SWAP = (2, 4)
@@ -25,7 +25,7 @@
 
 def moe_kernel(
     dims, x_ref, ids_ref, gates_ref, w1_ref, w3_ref, w2_ref, out_ref,
-    slot_ref, sgate_ref, dense, xall, xnb, smap, grecv, place, sbuf, drecv, rrecv, prcv, zret, acc, hbuf, gb, wb1, wb3, wb2,
+    slot_ref, sgate_ref, xall, xnb, smap, grecv, place, sbuf, drecv, rrecv, prcv, zret, acc, hbuf, gb, wb1, wb3, wb2,
     x_sem, w_sem, zs_send, zs_recv, sm_send, sm_recv, g_send, g_recv, e_send, e_recv, d_send, d_recv, r_send, r_recv,
     p_send, p_recv, zr_send, zr_recv,
 ):
@@ -33,7 +33,7 @@
     nq = ny * nx
     ndev = nz * nq
     tok, hid = xall.shape[1:]
-    cap = sbuf.shape[3]
+    cap = sbuf.shape[2]
     ff = wb1.shape[2]
     rows = nq * cap
     nt = 256
@@ -77,9 +77,7 @@
         return pl.ds((2 * g + h) * quarter, quarter)
 
     def tiles(h, g, body):
-        @pl.loop(0, quarter // nt)
-        def _(n):
-            body(pl.ds(pl.multiple_of((2 * g + h) * quarter + n * nt, nt), nt))
+        body(part(h, g))
 
     def weight_copies(e, slot):
         return (
@@ -130,7 +128,7 @@
     def d_copy(s, h, g, src, i):
         k = chunk[s]
         to = drecv.at[k, source(0, g, src), :, part(h, g)]
-        return rcopy(sbuf.at[s % 2, src, i, :, part(h, g)], to, d_send.at[s % 2, h], d_recv.at[k, h], at(z, peer(LAST[g][i])))
+        return rcopy(sbuf.at[src, i, :, part(h, g)], to, d_send.at[h], d_recv.at[k, h], at(z, peer(LAST[g][i])))
 
     def r_copy(s, h, g, src, i):
         k, f = chunk[s], LAST[g][i]
@@ -149,7 +147,7 @@
         pair(zret, zr_send.at[0, h], zr_recv.at[slot, h]).wait_recv()
 
     def summed(k, g, src, cols):
-        got = rrecv[k, src, :, :, cols].reshape(4 * cap, nt)
+        got = rrecv[k, src, :, :, cols].reshape(4 * cap, quarter)
         return lax.dot_general(place[k, 2 * g + src], got, (((0,), (0,)), ((), ())), preferred_element_type=F32)
 
     def swap_rows(s, h):
@@ -181,8 +179,8 @@
     def pick(s, h):
         k = chunk[s]
         pair(xnb, e_send.at[s, h], e_recv.at[k, h]).wait_recv()
-        if s >= 2:
-            blocks(6, d_send.at[s % 2, h], d_recv.at[k, h]).wait_send()
+        if s >= 1:
+            blocks(6, d_send.at[h], d_recv.at[k, h]).wait_send()
         if s not in placed:
             placed.add(s)
             tables(smap.at[k], 3 if s else 2, sm_send, sm_recv.at[k]).wait_recv()
@@ -198,16 +196,18 @@
 
                 def tile(cols, g=g, src=src, rows_of=rows_of):
                     got = jnp.dot(place[k, 2 * g + src], rows_of[k, :, cols], preferred_element_type=F32).astype(BF16)
-                    sbuf[s % 2, src, :, :, cols] = got.reshape(4, cap, nt)
-                    drecv[k, source(0, g, src), :, cols] = sbuf[s % 2, src, 0, :, cols]
+                    sbuf[src, :, :, cols] = got.reshape(4, cap, quarter)
+                    drecv[k, source(0, g, src), :, cols] = sbuf[src, 0, :, cols]
 
                 tiles(h, g, tile)
-                for i in range(1, 4):
+        for i in range(1, 4):
+            for g in range(2):
+                for src in range(2):
                     d_copy(s, h, g, src, i).start()
 
     def d_wait(k):
         for h in range(2):
-            blocks(6, d_send.at[0, h], d_recv.at[k, h]).wait_recv()
+            blocks(6, d_send.at[h], d_recv.at[k, h]).wait_recv()
 
     def send_back(s, h):
         k = chunk[s]
@@ -234,6 +234,7 @@
                 xnb[k, :, cols] = summed(k, g, 1, cols).astype(BF16)
 
             tiles(h, g, tile)
+        for g in range(2):
             p_copy(s, h, g).start()
 
     def pass_on(s, h):
@@ -284,6 +285,7 @@
                     xall[k, :, cols] = (own(g, cols) + zret[slot, :, cols].astype(F32)).astype(BF16)
 
                 tiles(h, g, tile)
+            for g in range(2):
                 zr_copy(k, h, g, s, z, k).start()
 
         @pl.when(inner == 0)
@@ -312,11 +314,11 @@
         gate = jnp.zeros((ndev * 8, tok), F32)
         for j in range(ids_ref.shape[0]):
             gate = gate + jnp.where(ids_ref[j : j + 1, :] == expert, gates_ref[j : j + 1, :], 0.0)
-        dense[...] = gate
+        acc[0 : ndev * 8, 0:tok] = gate
 
         @pl.loop(0, ndev, unroll=4)
         def _(d):
-            g = dense[pl.ds(pl.multiple_of(d * 8, 8), 8), :]
+            g = acc[pl.ds(pl.multiple_of(d * 8, 8), 8), 0:tok]
             hi = g.astype(BF16).astype(F32)
             mid = (g - hi).astype(BF16).astype(F32)
             low = g - hi - mid
@@ -455,8 +457,8 @@
             pair(xnb, p_send.at[s, h], p_recv.at[0, h]).wait_send()
             if s:
                 pair(xall, zr_send.at[s, h], zr_recv.at[0, h]).wait_send()
-            if s >= 2:
-                blocks(6, d_send.at[s % 2, h], d_recv.at[0, h]).wait_send()
+            if s == 3:
+                blocks(6, d_send.at[h], d_recv.at[0, h]).wait_send()
             blocks(6, r_send.at[s, h], r_recv.at[0, h]).wait_send()
     tables(sgate_ref, ndev - 1, g_send, g_recv).wait_send()
     tables(sgate_ref, 2 * (3 * nz - 1), sm_send, sm_recv.at[0]).wait_send()
@@ -479,13 +481,12 @@
         scratch_shapes=[
             pltpu.VMEM((nz, nq, tok), jnp.int32),
             pltpu.VMEM((ndev, 8, 128), F32),
-            pltpu.VMEM((ndev * 8, tok), F32),
             pltpu.VMEM((nz, tok, hid), BF16),
             pltpu.VMEM((nz, tok, hid), BF16),
             pltpu.VMEM((nz, 3, nq, tok), jnp.int32),
             pltpu.VMEM((ndev, 8, 128), F32),
             pltpu.VMEM((nz, 4, 4 * capacity, tok), BF16),
-            pltpu.VMEM((2, 2, 4, capacity, hid), BF16),
+            pltpu.VMEM((2, 4, capacity, hid), BF16),
             pltpu.VMEM((nz, nq, capacity, hid), BF16),
             pltpu.VMEM((nz, 2, 4, capacity, hid), BF16),
             pltpu.VMEM((nz, tok, hid), BF16),
@@ -506,7 +507,7 @@
             dma,
             dma((nz, 2)),
             dma((nz, 2)),
-            dma((2, 2)),
+            dma((2,)),
             dma((nz, 2)),
             dma((nz, 2)),
             dma((nz, 4)),

time: 213 us -> 206 us (0.967)
  Pallas kernels: 210 us -> 204 us
    pallas_call x1, Pallas kernels: 210 us -> 204 us  [moe_call(): pl.pallas_call(functools.partial(moe_kernel, dims), out_shape=jax.ShapeDt...]
where the time goes in v6:
time: 206 us
  Pallas kernels  204 us (99%)
  local copies, waits for them, and re-layouts  2.3 us (1%)
    pallas_call x1, Pallas kernels, moe_call(): pl.pallas_call(functools.partial(moe_kernel, dims), out_shape=jax.ShapeDt...  204 us

profile of v6, /device:TPU:0, one launch (start us, length us, event | category | flops | bytes accessed | tf_op | source)
XLA Modules:
  0.0 206.1 jit_solution(6215142616074243209)
XLA Ops:
  0.0 203.8 %shard_map.64 = bf16[256,2048]{1,0:T(8,128)(2,1)} custom-call(bf16[256,2048]{1,0:T(8,128)(2,1)} %x_ref.1, s32[8,256]{1,0:T(8,128)} %bitcast.2, f32[8,256]{1,0:T(8,128)} %bitcast.3, bf16[4,2048,768]{2,1,0:T(8,128)(2,1)} %w1_ref.1, bf16[4,2048,768]{2,1,0:T(8,128)(2,1)} %w3_ref.1, bf16[4,768,2048]{2,1,0:T(8,128)(2,1)} %w2_ref.1), custom_call_target="tpu_custom_call" | custom-call | tf_op jit(solution)/shard_map/pallas_call | solution.py:476
  203.8 2.3 %copy.8 = bf16[256,2048]{1,0:T(8,128)(2,1)} copy(bf16[256,2048]{1,0:T(8,128)(2,1)} %shard_map.64) | data formatting | bytes 2097152
